TPU v7x, 256 devices: a whole 4x4x8 slice. The times are simulated.
256 devices in a mesh: patch: 8 (over x, core), space: 32 (over z, y).
Axes of the slice: x: 4, y: 4, z: 8, core: 2. Of those that a mesh axis runs over, the one named last changes fastest.
Arguments:
- image: bfloat16 [64, 64, 256], P('patch', 'space'), may hold values from -6 to 6
- offsets: int32 [8, 2], replicated, may hold values from 0 to 128, as said below
- conv1_weight: bfloat16 [9, 32, 3], replicated, may hold values from -1.25 to 1.25
- conv2_weight: bfloat16 [9, 32, 96], replicated, may hold values from -0.21875 to 0.21875
- norm1_gain: float32 [32], replicated, may hold values from 0.1 to 1.9
- norm1_bias: float32 [32], replicated, may hold values from -3 to 3
- norm2_gain: float32 [32], replicated, may hold values from 0.1 to 1.9
- norm2_bias: float32 [32], replicated, may hold values from -3 to 3
- head_weight: bfloat16 [3, 32], replicated, may hold values from -1 to 1
- head_bias: float32 [3], replicated, may hold values from -3 to 3
Outputs:
- volume_logits: float32 [64, 3, 64, 256], P('patch', None, 'space')
Inputs may be any that keep to these rules, and one draw needn't show every extreme that they name: offsets[p] = (oz, ox) with 0 <= oz <= 48 and 0 <= ox <= 128; some patch starts at oz = 48, some at ox = 128, some at ox = 0.
All inputs are finite; a program needn't handle non-finite values.
Results may differ from a plain program's by a relative error of at most 0.0024.
Values may be sent and summed in bfloat16 or wider, within the bound.
A program may use at most 64 MiB of HBM per device.

v0:
```python
import jax
import jax.numpy as jnp
from jax import lax
from jax.sharding import PartitionSpec as P

PX = 128
PZ = 16


def padded_2(cells, sides, width):
    for axis, dim in sides:
        count = lax.axis_size(axis)
        ends = count - 1
        head = lax.slice_in_dim(cells, 0, width, axis=dim)
        tail = lax.slice_in_dim(cells, cells.shape[dim] - width, cells.shape[dim], axis=dim)
        cells = jnp.concatenate(
            [
                lax.ppermute(tail, axis, [(i, (i + 1) % count) for i in range(ends)]),
                cells,
                lax.ppermute(head, axis, [((i + 1) % count, i) for i in range(ends)]),
            ],
            axis=dim,
        )
    return cells


def copy_for_each(value, axis):
    copies = jnp.broadcast_to(value, (lax.axis_size(axis), *value.shape))
    return lax.all_to_all(copies, axis, split_axis=0, concat_axis=0, tiled=True)


def taken_together(value, axis):
    everything = copy_for_each(value, axis)
    return jnp.sum(everything, axis=0)


def in_one(arrays, axis):
    flat, at, finished = (jnp.concatenate([a.reshape(-1) for a in arrays]), 0, [])
    so_far = taken_together(flat, axis)
    for a in arrays:
        finished.append(so_far[at : at + a.size].reshape(a.shape))
        at += a.size
    return tuple(finished)


def joined_along(blocks, dim):
    blocks = jnp.moveaxis(blocks, 0, dim)
    dims = blocks.shape
    return blocks.reshape(*dims[:dim], dims[dim] * dims[dim + 1], *dims[dim + 2 :])


def gathered_copies(value, axis, dim):
    return joined_along(copy_for_each(value, axis), dim)


def in_blocks(value, dim, size):
    before, after = (value.shape[:dim], value.shape[dim + 1 :])
    return jnp.moveaxis(value.reshape(*before, size, -1, *after), dim, 0)


def summed_on_arrival(value, axis, dim):
    size = lax.axis_size(axis)
    blocks = lax.all_to_all(in_blocks(value, dim, size), axis, 0, 0, tiled=True)
    return jnp.sum(blocks, axis=0)


def gauss_value(positions, length):
    center = (length - 1) / 2.0
    deviation = length / 8.0
    offset = positions - center
    return jnp.exp(-(offset * offset) / (2.0 * deviation * deviation))


def apply_taps(padded, weights):
    depth_cells = padded.shape[2] - 2
    row_cells = padded.shape[3] - 2
    col_cells = padded.shape[4] - 2
    stacked = jnp.concatenate(
        [padded[:, :, :, :, col_shift : col_shift + col_cells] for col_shift in range(3)], axis=1
    )
    summed = jnp.zeros(
        (padded.shape[0], weights.shape[1], depth_cells, row_cells, col_cells), jnp.float32
    )
    for depth_tap in range(3):
        for row_tap in range(3):
            window = stacked[
                :, :, depth_tap : depth_tap + depth_cells, row_tap : row_tap + row_cells, :
            ]
            summed = summed + jnp.einsum(
                "oc,fczyx->fozyx",
                weights[depth_tap * 3 + row_tap],
                window,
                preferred_element_type=jnp.float32,
            )
    return summed


def convolve(features, weights):
    bordered = padded_2(features, (("space", 3),), 1)
    padded = jnp.pad(bordered, ((0, 0), (0, 0), (1, 1), (0, 0), (1, 1)))
    return apply_taps(padded, weights)


def normalize(values, channel_gain, channel_bias, cell_count):
    firsts, seconds = in_one(
        (jnp.sum(values, axis=(2, 3, 4)), jnp.sum(values * values, axis=(2, 3, 4))), "space"
    )
    average = firsts / cell_count
    variance = seconds / cell_count - average * average
    centered = values - average[:, :, None, None, None]
    factor = lax.rsqrt(variance + 1e-05) * channel_gain[None, :]
    shifted = centered * factor[:, :, None, None, None] + channel_bias[None, :, None, None, None]
    return jnp.where(shifted >= 0, shifted, 0.01 * shifted).astype(jnp.bfloat16)


def place_patch(contrib, corner, first_row, row_count, width_cells):
    padded = jnp.pad(
        contrib, ((row_count, row_count), (0, 0), (0, 0), (width_cells - PX, width_cells - PX))
    )
    first_slot = jnp.clip(first_row - corner[0] + row_count, 0, PZ + row_count)
    picked = lax.dynamic_slice_in_dim(padded, first_slot, row_count, 0)
    return lax.dynamic_slice_in_dim(picked, width_cells - PX - corner[1], width_cells, 3)


def local(
    image,
    offsets,
    conv1_weight,
    conv2_weight,
    norm1_gain,
    norm1_bias,
    norm2_gain,
    norm2_bias,
    head_weight,
    head_bias,
):
    groups = lax.axis_size("patch")
    group_index = lax.axis_index("patch")
    spaces = lax.axis_size("space")
    band_index = lax.axis_index("space")
    slab_rows = image.shape[0]
    band_rows = image.shape[1]
    width_cells = image.shape[2]
    patch_rows = band_rows * spaces
    per_group = offsets.shape[0] // groups
    own_corners = lax.dynamic_slice_in_dim(offsets, group_index * per_group, per_group, 0)
    shard_part = gathered_copies(image, "patch", 0)
    row_count = shard_part.shape[0]
    padded = jnp.pad(shard_part, ((PZ, PZ), (0, 0), (0, 0)))

    def one_corner(corner):
        first_slot = jnp.clip(corner[0] + PZ, 0, row_count + PZ)
        picked = lax.dynamic_slice_in_dim(padded, first_slot, PZ, 0)
        return lax.dynamic_slice_in_dim(picked, corner[1], PX, 2)

    patches = jax.vmap(one_corner)(own_corners)
    gauss_depth = gauss_value(jnp.arange(PZ, dtype=jnp.float32), PZ)
    band_positions = (band_index * band_rows + jnp.arange(band_rows, dtype=jnp.int32)).astype(
        jnp.float32
    )
    gauss_band = gauss_value(band_positions, patch_rows)
    gauss_cols = gauss_value(jnp.arange(PX, dtype=jnp.float32), PX)
    weight_map = gauss_depth[:, None, None] * gauss_band[None, :, None] * gauss_cols[None, None, :]
    cell_count = float(PZ * patch_rows * PX)

    def one_patch(patch_cells):
        flipped = jnp.stack(
            [patch_cells, patch_cells[::-1], patch_cells[:, :, ::-1], patch_cells[::-1, :, ::-1]]
        )[:, None]
        hidden = normalize(convolve(flipped, conv1_weight), norm1_gain, norm1_bias, cell_count)
        hidden = normalize(convolve(hidden, conv2_weight), norm2_gain, norm2_bias, cell_count)
        logits = jnp.einsum(
            "kc,fczyx->fzkyx", head_weight, hidden, preferred_element_type=jnp.float32
        )
        logits = logits + head_bias[None, None, :, None, None]
        restored = (
            logits[0] + logits[1][::-1] + logits[2][:, :, :, ::-1] + logits[3][::-1, :, :, ::-1]
        )
        return restored * 0.25 * weight_map[:, None, :, :]

    contribs = lax.map(one_patch, patches)
    first_row = jnp.int32(0)

    def place_one(contrib, corner):
        return place_patch(
            contrib, corner, first_row, slab_rows * lax.axis_size("patch"), width_cells
        )

    blended = summed_on_arrival(
        jnp.sum(jax.vmap(place_one)(contribs, own_corners), axis=0), "patch", 0
    )
    slab_positions = group_index * slab_rows + jnp.arange(slab_rows, dtype=jnp.int32)
    rel_depth = slab_positions[None, :] - offsets[:, 0:1]
    depth_weights = jnp.where(
        (rel_depth >= 0) & (rel_depth < PZ), gauss_value(rel_depth.astype(jnp.float32), PZ), 0.0
    )
    col_positions = jnp.arange(width_cells, dtype=jnp.int32)
    rel_cols = col_positions[None, :] - offsets[:, 1:2]
    col_weights = jnp.where(
        (rel_cols >= 0) & (rel_cols < PX), gauss_value(rel_cols.astype(jnp.float32), PX), 0.0
    )
    plane = jnp.dot(
        depth_weights.T,
        col_weights,
        precision=lax.Precision.HIGHEST,
        preferred_element_type=jnp.float32,
    )
    coverage = plane[:, None, :] * gauss_band[None, :, None]
    return blended / jnp.maximum(coverage, 0.1)[:, None, :, :]


def solution(mesh):
    return jax.shard_map(
        local,
        mesh=mesh,
        in_specs=(P("patch", "space", None), P(), P(), P(), P(), P(), P(), P(), P(), P()),
        out_specs=P("patch", None, "space", None),
        check_vma=False,
    )
```

profile of v0, /device:TPU:1, one launch (start us, length us, event | category | flops | bytes accessed | tf_op | source)
XLA Modules:
  0.0 114.9 jit_solution(12276318690431048073)
XLA Ops:
  0.0 0.7 copy.40
  1.4 6.5 %all-to-all-start = ((bf16[8,8,2,256]{3,1,2,0:T(8,128)(2,1)}), bf16[8,8,2,256]{3,1,2,0:T(8,128)(2,1)S(1)}, u32[]{:S(2)}, u32[]{:S(2)}) async-start(bf16[8,8,2,256]{3,1,2,0:T(8,128)(2,1)} %broadcast_in_dim.65), calls=%async_computation | async-start | bytes 131072 | tf_op jit(solution)/shard_map/all_to_all | solution.py:29
  7.8 0.8 slice_bitcast_fusion.5
  8.6 0.7 constant_dynamic-slice_fusion
  13.3 2.5 %collective-permute-start = (bf16[4,1,16,1,128]{4,1,3,2,0:T(2,128)(2,1)S(1)}, bf16[4,1,16,1,128]{4,1,3,2,0:T(2,128)(2,1)S(1)}, u32[]{:S(2)}, u32[]{:S(2)}) collective-permute-start(bf16[4,1,16,1,128]{4,1,3,2,0:T(2,128)(2,1)S(1)} %get-tuple-element.100), channel_id=1, source_target_pairs={{0,1},{1,2},{2,3},{3,4},{4,5},{5,6},{6,7},{7,8},{8,9},{9,10},{10,1... | collective-permute-start | bytes 49160 | tf_op jit(solution)/shard_map/while/body/eval_jaxpr/ppermute | solution.py:18
  15.8 1.3 %collective-permute-start.1 = (bf16[4,1,16,1,128]{4,1,3,2,0:T(2,128)(2,1)S(1)}, bf16[4,1,16,1,128]{4,1,3,2,0:T(2,128)(2,1)S(1)}, u32[]{:S(2)}, u32[]{:S(2)}) collective-permute-start(bf16[4,1,16,1,128]{4,1,3,2,0:T(2,128)(2,1)S(1)} %get-tuple-element.101), channel_id=1, source_target_pairs={{1,0},{2,1},{3,2},{4,3},{5,4},{6,5},{7,6},{8,7},{9,8},{10,9},{11,1... | collective-permute-start | bytes 49160 | tf_op jit(solution)/shard_map/while/body/eval_jaxpr/ppermute | solution.py:20
  19.1 1.4 %collective-permute-done.1 = bf16[4,1,16,1,128]{4,1,3,2,0:T(2,128)(2,1)S(1)} collective-permute-done((bf16[4,1,16,1,128]{4,1,3,2,0:T(2,128)(2,1)S(1)}, bf16[4,1,16,1,128]{4,1,3,2,0:T(2,128)(2,1)S(1)}, u32[]{:S(2)}, u32[]{:S(2)}) %collective-permute-start.1) | collective-permute-done | bytes 16416 | tf_op jit(solution)/shard_map/while/body/eval_jaxpr/ppermute | solution.py:20
  25.5 1.6 %bitcast_reduce_fusion.1 = (f32[4,32]{1,0:T(4,128)S(1)}, f32[4,32]{1,0:T(4,128)S(1)}, f32[4,16,2,128,32]{3,4,2,1,0:T(8,128)S(1)}) fusion(bf16[9,32,3]{1,2,0:T(4,128)(2,1)S(1)} %copy-done.2, f32[4,16,2,128,32]{3,4,2,1,0:T(8,128)S(1)} %fusion.96, f32[4,16,2,128,32]{3,4,2,1,0:T(8,128)S(1)} %fusion.98, f32[4,16,2,128,32]{3,4,2,1,0:T(8,128)S(1)} %fusion.100, ...), kind=kOutput, calls=%fused_computation.43 | convolution fusion | flops 9576192 | bytes 19318784 | tf_op jit(solution)/shard_map/while/body/eval_jaxpr/oc,fczyx->fozyx/dot_general | solution.py:89
  27.9 13.0 %all-to-all-start.1 = ((f32[32,1,256]{2,1,0:T(1,128)}), f32[32,1,256]{2,1,0:T(1,128)S(1)}, u32[]{:S(2)}, u32[]{:S(2)}) async-start(f32[32,1,256]{2,1,0:T(1,128)} %broadcast_in_dim.68), calls=%async_computation.1 | async-start | bytes 65536 | tf_op jit(solution)/shard_map/while/body/eval_jaxpr/all_to_all | solution.py:29
  40.9 8.7 %all-to-all-done.1 = f32[32,1,256]{2,1,0:T(1,128)S(1)} async-done(((f32[32,1,256]{2,1,0:T(1,128)}), f32[32,1,256]{2,1,0:T(1,128)S(1)}, u32[]{:S(2)}, u32[]{:S(2)}) %all-to-all-start.1) | async-done | bytes 32800 | tf_op jit(solution)/shard_map/while/body/eval_jaxpr/all_to_all | solution.py:29
  49.9 0.7 fusion.24
  50.7 2.2 %collective-permute-start.2 = (bf16[4,32,16,1,128]{4,1,3,2,0:T(8,128)(2,1)S(1)}, bf16[4,32,16,1,128]{4,1,3,2,0:T(8,128)(2,1)S(1)}, u32[]{:S(2)}, u32[]{:S(2)}) collective-permute-start(bf16[4,32,16,1,128]{4,1,3,2,0:T(8,128)(2,1)S(1)} %get-tuple-element.92), channel_id=1, source_target_pairs={{0,1},{1,2},{2,3},{3,4},{4,5},{5,6},{6,7},{7,8},{8,9},{9,10},{10,1... | collective-permute-start | bytes 1572872 | tf_op jit(solution)/shard_map/while/body/eval_jaxpr/ppermute | solution.py:18
  52.9 1.5 %collective-permute-start.3 = (bf16[4,32,16,1,128]{4,1,3,2,0:T(8,128)(2,1)S(1)}, bf16[4,32,16,1,128]{4,1,3,2,0:T(8,128)(2,1)S(1)}, u32[]{:S(2)}, u32[]{:S(2)}) collective-permute-start(bf16[4,32,16,1,128]{4,1,3,2,0:T(8,128)(2,1)S(1)} %get-tuple-element.93), channel_id=1, source_target_pairs={{1,0},{2,1},{3,2},{4,3},{5,4},{6,5},{7,6},{8,7},{9,8},{10,9},{11,1... | collective-permute-start | bytes 1572872 | tf_op jit(solution)/shard_map/while/body/eval_jaxpr/ppermute | solution.py:20
  54.6 5.9 %collective-permute-done.2 = bf16[4,32,16,1,128]{4,1,3,2,0:T(8,128)(2,1)S(1)} collective-permute-done((bf16[4,32,16,1,128]{4,1,3,2,0:T(8,128)(2,1)S(1)}, bf16[4,32,16,1,128]{4,1,3,2,0:T(8,128)(2,1)S(1)}, u32[]{:S(2)}, u32[]{:S(2)}) %collective-permute-start.2) | collective-permute-done | bytes 524320 | tf_op jit(solution)/shard_map/while/body/eval_jaxpr/ppermute | solution.py:18
  60.5 3.9 %collective-permute-done.3 = bf16[4,32,16,1,128]{4,1,3,2,0:T(8,128)(2,1)S(1)} collective-permute-done((bf16[4,32,16,1,128]{4,1,3,2,0:T(8,128)(2,1)S(1)}, bf16[4,32,16,1,128]{4,1,3,2,0:T(8,128)(2,1)S(1)}, u32[]{:S(2)}, u32[]{:S(2)}) %collective-permute-start.3) | collective-permute-done | bytes 524320 | tf_op jit(solution)/shard_map/while/body/eval_jaxpr/ppermute | solution.py:20
  64.4 2.7 %select_maximum_fusion = bf16[4,32,18,4,130]{4,1,3,2,0:T(8,128)(2,1)S(1)} fusion(bf16[4,32,16,1,128]{4,1,3,2,0:T(8,128)(2,1)S(1)} %collective-permute-done.3, bf16[4,32,16,2,128]{4,1,3,2,0:T(8,128)(2,1)S(1)} %fusion.24, bf16[4,32,16,1,128]{4,1,3,2,0:T(8,128)(2,1)S(1)} %collective-permute-done.2), kind=kLoop, calls=%fused_computation.10 | loop fusion | flops 22763520 | bytes 4493312 | tf_op jit(solution)/shard_map/while/body/eval_jaxpr/concatenate | solution.py:16
  67.1 1.9 %fusion.131 = (bf16[4,32,18,4,128]{4,1,3,2,0:T(8,128)(2,1)S(1)}, bf16[4,32,18,4,128]{4,1,3,2,0:T(8,128)(2,1)S(1)}, bf16[4,32,18,4,128]{4,1,3,2,0:T(8,128)(2,1)S(1)}) fusion(bf16[4,32,18,4,130]{4,1,3,2,0:T(8,128)(2,1)S(1)} %select_maximum_fusion), kind=kLoop, calls=%fused_computation.178 | loop fusion | bytes 14155776 | tf_op jit(solution)/shard_map/while/body/eval_jaxpr/slice | solution.py:79
  69.0 0.8 pad_maximum_fusion
  74.3 1.5 %bitcast_reduce_fusion = (f32[4,32]{1,0:T(4,128)S(1)}, f32[4,32]{1,0:T(4,128)S(1)}, f32[4,16,2,128,32]{3,4,2,1,0:T(8,128)S(1)}) fusion(bf16[4,96,18,4,128]{4,1,3,2,0:T(8,128)(2,1)S(1)} %pad_maximum_fusion, bf16[9,32,96]{2,1,0:T(8,128)(2,1)S(1)} %copy-done.1, f32[4,16,2,128,32]{3,4,2,1,0:T(8,128)S(1)} %fusion.8, f32[4,16,2,128,32]{3,4,2,1,0:T(8,128)S(1)} %fusion.10, ...), kind=kOutput, calls=%fused_computation.37 | convolution fusion | flops 106430208 | bytes 22029312 | tf_op jit(solution)/shard_map/while/body/eval_jaxpr/oc,fczyx->fozyx/dot_general | solution.py:89
  76.7 8.2 %all-to-all-start.2 = ((f32[32,1,256]{2,1,0:T(1,128)}), f32[32,1,256]{2,1,0:T(1,128)S(1)}, u32[]{:S(2)}, u32[]{:S(2)}) async-start(f32[32,1,256]{2,1,0:T(1,128)} %broadcast_in_dim.69), calls=%async_computation.2 | async-start | bytes 65536 | tf_op jit(solution)/shard_map/while/body/eval_jaxpr/all_to_all | solution.py:29
  84.8 8.7 %all-to-all-done.2 = f32[32,1,256]{2,1,0:T(1,128)S(1)} async-done(((f32[32,1,256]{2,1,0:T(1,128)}), f32[32,1,256]{2,1,0:T(1,128)S(1)}, u32[]{:S(2)}, u32[]{:S(2)}) %all-to-all-start.2) | async-done | bytes 32800 | tf_op jit(solution)/shard_map/while/body/eval_jaxpr/all_to_all | solution.py:29
  95.4 0.9 copy.48
  96.2 10.2 %all-to-all-start.3 = ((f32[8,8,3,2,256]{4,1,3,2,0:T(8,128)}), f32[8,8,3,2,256]{4,1,3,2,0:T(8,128)S(1)}, u32[]{:S(2)}, u32[]{:S(2)}) async-start(f32[8,8,3,2,256]{4,1,3,2,0:T(8,128)} %copy.48), calls=%async_computation.3 | async-start | bytes 786432 | tf_op jit(solution)/shard_map/all_to_all | solution.py:63
  106.8 7.3 %all-to-all-done.3 = f32[8,8,3,2,256]{4,1,3,2,0:T(8,128)S(1)} async-done(((f32[8,8,3,2,256]{4,1,3,2,0:T(8,128)}), f32[8,8,3,2,256]{4,1,3,2,0:T(8,128)S(1)}, u32[]{:S(2)}, u32[]{:S(2)}) %all-to-all-start.3) | async-done | bytes 393248 | tf_op jit(solution)/shard_map/all_to_all | solution.py:63
  (83 shorter events, 16.5 us)
Async XLA Ops:
  0.0 93.8 %copy-start = (bf16[3,32]{1,0:T(4,128)(2,1)S(1)}, bf16[3,32]{1,0:T(4,128)(2,1)}, u32[]{:S(2)}) copy-start(bf16[3,32]{1,0:T(4,128)(2,1)} %param.18) | copy-start | bytes 580
  0.0 21.6 %copy-start.2 = (bf16[9,32,3]{1,2,0:T(4,128)(2,1)S(1)}, bf16[9,32,3]{1,2,0:T(4,128)(2,1)}, u32[]{:S(2)}) copy-start(bf16[9,32,3]{1,2,0:T(4,128)(2,1)} %param.12) | copy-start | bytes 5188
  1.4 11.3 %all-to-all-start = ((bf16[8,8,2,256]{3,1,2,0:T(8,128)(2,1)}), bf16[8,8,2,256]{3,1,2,0:T(8,128)(2,1)S(1)}, u32[]{:S(2)}, u32[]{:S(2)}) async-start(bf16[8,8,2,256]{3,1,2,0:T(8,128)(2,1)} %broadcast_in_dim.65), calls=%async_computation | async-start | bytes 131072 | tf_op jit(solution)/shard_map/all_to_all | solution.py:29
  13.3 5.8 %collective-permute-start = (bf16[4,1,16,1,128]{4,1,3,2,0:T(2,128)(2,1)S(1)}, bf16[4,1,16,1,128]{4,1,3,2,0:T(2,128)(2,1)S(1)}, u32[]{:S(2)}, u32[]{:S(2)}) collective-permute-start(bf16[4,1,16,1,128]{4,1,3,2,0:T(2,128)(2,1)S(1)} %get-tuple-element.100), channel_id=1, source_target_pairs={{0,1},{1,2},{2,3},{3,4},{4,5},{5,6},{6,7},{7,8},{8,9},{9,10},{10,1... | collective-permute-start | bytes 49160 | tf_op jit(solution)/shard_map/while/body/eval_jaxpr/ppermute | solution.py:18
  15.8 4.7 %collective-permute-start.1 = (bf16[4,1,16,1,128]{4,1,3,2,0:T(2,128)(2,1)S(1)}, bf16[4,1,16,1,128]{4,1,3,2,0:T(2,128)(2,1)S(1)}, u32[]{:S(2)}, u32[]{:S(2)}) collective-permute-start(bf16[4,1,16,1,128]{4,1,3,2,0:T(2,128)(2,1)S(1)} %get-tuple-element.101), channel_id=1, source_target_pairs={{1,0},{2,1},{3,2},{4,3},{5,4},{6,5},{7,6},{8,7},{9,8},{10,9},{11,1... | collective-permute-start | bytes 49160 | tf_op jit(solution)/shard_map/while/body/eval_jaxpr/ppermute | solution.py:20
  25.5 24.4 %copy-start.3 = (f32[32]{0:T(128)S(1)}, f32[32]{0:T(128)}, u32[]{:S(2)}) copy-start(f32[32]{0:T(128)} %param.14) | copy-start | bytes 388
  25.5 24.3 %copy-start.5 = (f32[32]{0:T(128)S(1)}, f32[32]{0:T(128)}, u32[]{:S(2)}) copy-start(f32[32]{0:T(128)} %param.15) | copy-start | bytes 388
  27.9 21.7 %all-to-all-start.1 = ((f32[32,1,256]{2,1,0:T(1,128)}), f32[32,1,256]{2,1,0:T(1,128)S(1)}, u32[]{:S(2)}, u32[]{:S(2)}) async-start(f32[32,1,256]{2,1,0:T(1,128)} %broadcast_in_dim.68), calls=%async_computation.1 | async-start | bytes 65536 | tf_op jit(solution)/shard_map/while/body/eval_jaxpr/all_to_all | solution.py:29
  50.7 9.8 %collective-permute-start.2 = (bf16[4,32,16,1,128]{4,1,3,2,0:T(8,128)(2,1)S(1)}, bf16[4,32,16,1,128]{4,1,3,2,0:T(8,128)(2,1)S(1)}, u32[]{:S(2)}, u32[]{:S(2)}) collective-permute-start(bf16[4,32,16,1,128]{4,1,3,2,0:T(8,128)(2,1)S(1)} %get-tuple-element.92), channel_id=1, source_target_pairs={{0,1},{1,2},{2,3},{3,4},{4,5},{5,6},{6,7},{7,8},{8,9},{9,10},{10,1... | collective-permute-start | bytes 1572872 | tf_op jit(solution)/shard_map/while/body/eval_jaxpr/ppermute | solution.py:18
  52.9 11.5 %collective-permute-start.3 = (bf16[4,32,16,1,128]{4,1,3,2,0:T(8,128)(2,1)S(1)}, bf16[4,32,16,1,128]{4,1,3,2,0:T(8,128)(2,1)S(1)}, u32[]{:S(2)}, u32[]{:S(2)}) collective-permute-start(bf16[4,32,16,1,128]{4,1,3,2,0:T(8,128)(2,1)S(1)} %get-tuple-element.93), channel_id=1, source_target_pairs={{1,0},{2,1},{3,2},{4,3},{5,4},{6,5},{7,6},{8,7},{9,8},{10,9},{11,1... | collective-permute-start | bytes 1572872 | tf_op jit(solution)/shard_map/while/body/eval_jaxpr/ppermute | solution.py:20
  69.0 0.9 copy-start.1
  74.3 19.5 %copy-start.4 = (f32[32]{0:T(128)S(1)}, f32[32]{0:T(128)}, u32[]{:S(2)}) copy-start(f32[32]{0:T(128)} %param.16) | copy-start | bytes 388
  74.3 19.5 %copy-start.6 = (f32[32]{0:T(128)S(1)}, f32[32]{0:T(128)}, u32[]{:S(2)}) copy-start(f32[32]{0:T(128)} %param.17) | copy-start | bytes 388
  74.3 19.5 %copy-start.7 = (f32[3]{0:T(128)S(1)}, f32[3]{0:T(128)}, u32[]{:S(2)}) copy-start(f32[3]{0:T(128)} %param.19) | copy-start | bytes 40
  76.7 16.9 %all-to-all-start.2 = ((f32[32,1,256]{2,1,0:T(1,128)}), f32[32,1,256]{2,1,0:T(1,128)S(1)}, u32[]{:S(2)}, u32[]{:S(2)}) async-start(f32[32,1,256]{2,1,0:T(1,128)} %broadcast_in_dim.69), calls=%async_computation.2 | async-start | bytes 65536 | tf_op jit(solution)/shard_map/while/body/eval_jaxpr/all_to_all | solution.py:29
  96.2 17.9 %all-to-all-start.3 = ((f32[8,8,3,2,256]{4,1,3,2,0:T(8,128)}), f32[8,8,3,2,256]{4,1,3,2,0:T(8,128)S(1)}, u32[]{:S(2)}, u32[]{:S(2)}) async-start(f32[8,8,3,2,256]{4,1,3,2,0:T(8,128)} %copy.48), calls=%async_computation.3 | async-start | bytes 786432 | tf_op jit(solution)/shard_map/all_to_all | solution.py:63
where the time goes:
time: 116 us; the launch traced here: 115 us
  starting transfers between devices  45.3 us (39%)
  waiting for transfers between devices  36.1 us (31%)
  matrix products  12.3 us (11%)
  local copies, waits for them, and re-layouts  10.9 us (9%)
  other arithmetic  5.31 us (5%)
  between operations  4.89 us (4%)
    all_to_all x3, starting transfers between devices, copy_for_each(): return lax.all_to_all(copies, axis, split_axis=0, concat_axis=0, tiled=True)  27.6 us
    all_to_all x3, waiting for transfers between devices, copy_for_each(): return lax.all_to_all(copies, axis, split_axis=0, concat_axis=0, tiled=True)  17.6 us
    dot_general x18, matrix products, apply_taps(): jnp.einsum('oc,fczyx->fozyx', weights[depth_tap * 3 + row_tap], window, p...  11.4 us
    all_to_all x1, starting transfers between devices, summed_on_arrival(): blocks = lax.all_to_all(in_blocks(value, dim, size), axis, 0, 0, tiled=True)  10.2 us
    all_to_all x1, waiting for transfers between devices, summed_on_arrival(): blocks = lax.all_to_all(in_blocks(value, dim, size), axis, 0, 0, tiled=True)  7.35 us
    ppermute x2, waiting for transfers between devices, padded_2(): lax.ppermute(tail, axis, [(i, (i + 1) % count) for i in range(ends)])  5.94 us
    ppermute x2, waiting for transfers between devices, padded_2(): lax.ppermute(head, axis, [((i + 1) % count, i) for i in range(ends)])  5.25 us
    ppermute x2, starting transfers between devices, padded_2(): lax.ppermute(tail, axis, [(i, (i + 1) % count) for i in range(ends)])  4.76 us
  transfers between devices with their start and end apart: 8, of which 7 were waited for; matrix products, arithmetic and copies ran while one was open for 2% of the time, Pallas kernels for 0%

commit v1 on v0

v1 whole, which is shorter than its diff:
```python
import jax
import jax.numpy as jnp
from jax import lax
from jax.experimental import pallas as pl
from jax.experimental.pallas import tpu as pltpu
from jax.sharding import PartitionSpec as P

PX = 128
PZ = 16
CH = 32
NP = 8
NS = 32
PY = 64
VX = 256
MESH = pl.DeviceIdType.MESH
BF = jnp.bfloat16
F32 = jnp.float32
HI = lax.Precision.HIGHEST


def iota(shape, dim):
    return lax.broadcasted_iota(jnp.int32, shape, dim)


def gauss(positions, length):
    center = (length - 1) / 2.0
    deviation = length / 8.0
    offset = positions - center
    return jnp.exp(-(offset * offset) / (2.0 * deviation * deviation))


def kernel(
    image, offs, w1, w2, g1, b1, g2, b2, hw, hb, out,
    slab, xsend, gath, w1s, w2s, whs, sels, im2, own, halo, act, pbuf, conv, hid,
    st1, st2, unblend, place, inv, wmap, logit, msend, mrecv,
    s_img, r_img, s_st1, r_st1, s_st2, r_st2, s_out, r_out,
):
    me = lax.axis_index("patch")
    sp = lax.axis_index("space")

    def space(k):
        return lax.rem(sp + k + NS, NS)

    def group(k):
        return lax.rem(me + k, NP)

    barrier = pltpu.get_barrier_semaphore()

    def greet(p, s):
        pl.semaphore_signal(barrier, inc=1, device_id=(p, s), device_id_type=MESH)

    def greet_space(k, c):
        greet(me, space(k))
        return c

    lax.fori_loop(1, NS, greet_space, 0)

    def greet_group(k, c):
        greet(group(k), sp)
        greet(group(k), space(1))
        greet(group(k), space(-1))
        return c

    lax.fori_loop(1, NP, greet_group, 0)

    for z in range(8):
        slab[2 * z : 2 * z + 2, :] = image[z].astype(F32)
    diff = iota((VX, PX), 0) - iota((VX, PX), 1)
    for p in range(NP):
        pick = jnp.where(diff == offs[p, 1], 1.0, 0.0).astype(BF)
        xsend[p] = jnp.dot(slab[...].astype(BF), pick, preferred_element_type=F32).astype(BF)

    pl.semaphore_wait(barrier, NS - 1 + 3 * (NP - 1))

    def image_copy(n, p):
        return pltpu.make_async_remote_copy(
            src_ref=xsend.at[p], dst_ref=gath.at[n, me],
            send_sem=s_img.at[n, p], recv_sem=r_img.at[n, me],
            device_id=(p, space(1 - n)), device_id_type=MESH,
        )

    def image_arrival(n, q):
        return pltpu.make_async_remote_copy(
            src_ref=xsend.at[q], dst_ref=gath.at[n, q],
            send_sem=s_img.at[n, q], recv_sem=r_img.at[n, q],
            device_id=(q, space(1 - n)), device_id_type=MESH,
        )

    def send_images(k, c):
        image_copy(0, group(k)).start()
        image_copy(2, group(k)).start()
        image_copy(1, group(k)).start()
        return c

    lax.fori_loop(1, NP, send_images, 0)
    image_copy(0, me).start()
    image_copy(2, me).start()
    gath[1, me] = xsend[me]

    lane = iota((CH, VX), 1)
    for flip in range(2):
        base = jnp.zeros((CH, VX), F32)
        for a in range(3):
            for b in range(3):
                taps = w1[3 * a + b].astype(F32)
                for c in range(3):
                    where = c * 48 + b * 8 + (2 - a if flip else a)
                    base = base + jnp.where(lane == where, taps[:, c : c + 1], 0.0)
        for part in range(2):
            for zo in range(4):
                for r in range(2):
                    row = (1 + r) if part == 0 else 3 * r
                    shift = row * 8 + zo
                    moved = base if shift == 0 else pltpu.roll(base, shift, 1)
                    at = part * 512 + flip * 256 + zo * 64 + r * 32
                    w1s[at : at + 32, :] = moved[:, :144].astype(BF)
    nothing = jnp.zeros((CH, 96), F32)
    for a in range(3):
        taps = [w2[3 * a + b].astype(F32) for b in range(3)]
        for ro in range(2):
            pieces = [nothing] + taps if ro else taps + [nothing]
            block = jnp.concatenate(pieces, axis=1).astype(BF)
            for zp in range(2):
                slot = zp - a + 2
                if 0 <= slot < 4:
                    at = (slot * 2 + ro) * 32
                    w2s[at : at + 32, zp * 384 : zp * 384 + 384] = block
    for slot, zp in ((3, 0), (0, 1)):
        w2s[slot * 64 : slot * 64 + 64, zp * 384 : zp * 384 + 384] = jnp.zeros((64, 384), BF)

    oz = offs[me, 0]
    rows = iota((48, 384), 0)
    cols = iota((48, 384), 1)
    slot_n = lax.shift_right_logical(cols, 7)
    from_z = lax.shift_right_logical(cols & 127, 1)
    from_row = slot_n * 2 + (cols & 1)
    to_row = lax.shift_right_logical(rows, 3)
    low = jnp.where(sp == 0, 2, 0)
    high = jnp.where(sp == NS - 1, 3, 5)
    keep_row = (from_row == to_row) & (to_row >= low) & (to_row <= high)
    for b in range(4):
        rel = (rows & 7) + (4 * b - 1)
        hit = keep_row & (from_z == rel + oz) & (rel >= 0) & (rel < PZ)
        sels[b * 48 : b * 48 + 48, :] = jnp.where(hit, 1.0, 0.0).astype(BF)

    for n in range(3):
        def wait_image(q, c, n=n):
            image_arrival(n, q).wait_recv()
            return c
        if n == 1:
            lax.fori_loop(1, NP, lambda k, c: wait_image(group(k), c), 0)
        else:
            lax.fori_loop(0, NP, wait_image, 0)

    rowsel = jnp.dot(sels[...], gath[...].reshape(384, PX), preferred_element_type=F32)
    lane_r = iota((192, PX), 1)
    before = jnp.where(lane_r == 0, 0.0, pltpu.roll(rowsel, 1, 1))
    after = jnp.where(lane_r == PX - 1, 0.0, pltpu.roll(rowsel, PX - 1, 1))
    for c, cells in enumerate((before, rowsel, after)):
        for b in range(4):
            cut = cells[b * 48 : b * 48 + 48].astype(BF)
            im2[c * 48 : c * 48 + 48, b * PX : b * PX + PX] = cut
            im2[(2 - c) * 48 : (2 - c) * 48 + 48, 512 + b * PX : 512 + b * PX + PX] = cut

    def sums(parts):
        first = parts[0]
        second = parts[0] * parts[0]
        for part in parts[1:]:
            first = first + part
            second = second + part * part
        return first, second

    def to_lanes(blocks):
        cells = jnp.concatenate(blocks, axis=0)
        return jnp.sum(jnp.transpose(cells), axis=0, keepdims=True)

    own[...] = jnp.dot(w1s[:512], im2[...], preferred_element_type=F32)
    firsts, seconds = [], []
    for zf in range(2):
        for xf in range(2):
            one, two = sums([
                own[zf * 256 + i * 32 : zf * 256 + i * 32 + 32, xf * 512 + b * PX : xf * 512 + b * PX + PX]
                for i in range(8) for b in range(4)
            ])
            firsts.append(one)
            seconds.append(two)

    def stat_copy(buf, ssem, rsem, k):
        return pltpu.make_async_remote_copy(
            src_ref=buf.at[sp], dst_ref=buf.at[sp],
            send_sem=ssem.at[k], recv_sem=rsem.at[sp],
            device_id=(me, space(k)), device_id_type=MESH,
        )

    def stat_arrival(buf, ssem, rsem, k):
        return pltpu.make_async_remote_copy(
            src_ref=buf.at[space(k)], dst_ref=buf.at[space(k)],
            send_sem=ssem.at[k], recv_sem=rsem.at[space(k)],
            device_id=(me, space(k)), device_id_type=MESH,
        )

    def send_stats(buf, ssem, rsem):
        def body(k, c):
            stat_copy(buf, ssem, rsem, lax.rem(k + 15, NS - 1) + 1).start()
            return c
        lax.fori_loop(0, NS - 1, body, 0)

    def wait_stats(buf, ssem, rsem):
        def body(k, c):
            stat_arrival(buf, ssem, rsem, k).wait_recv()
            return c
        lax.fori_loop(1, NS, body, 0)

    def scales(buf, gain, bias):
        total = jnp.sum(buf[...], axis=0)
        cells = float(PZ * PY * PX)
        mean = total[0:1] / cells
        variance = total[1:2] / cells - mean * mean
        factor = lax.rsqrt(variance + 1e-05) * jnp.concatenate([gain[...]] * 4, axis=1)
        shift = jnp.concatenate([bias[...]] * 4, axis=1) - mean * factor
        return (
            jnp.transpose(jnp.broadcast_to(factor, (128, 128))),
            jnp.transpose(jnp.broadcast_to(shift, (128, 128))),
        )

    def leaky(u):
        return jnp.maximum(u, 0.01 * u)

    st1[sp] = jnp.concatenate([to_lanes(firsts), to_lanes(seconds)], axis=0)
    send_stats(st1, s_st1, r_st1)

    halo[...] = jnp.dot(w1s[512:], im2[...], preferred_element_type=F32)

    row16 = iota((16, 512), 0)
    col16 = iota((16, 512), 1)
    head = jnp.concatenate([hw[...].astype(F32)] * 16, axis=1)
    k16 = lax.shift_right_logical(row16 & 7, 1)
    spread = jnp.zeros((16, 512), F32)
    for k in range(3):
        spread = jnp.where(k16 == k, head[k : k + 1, :], spread)
    same = (lax.shift_right_logical(row16, 3) == (lax.shift_right_logical(col16, 6) & 1)) & (
        (row16 & 1) == (lax.shift_right_logical(col16, 5) & 1)
    )
    whs[...] = jnp.where(same, spread, 0.0).astype(BF)

    lead = iota((128, PX), 0)
    width = iota((128, PX), 1)
    row_y = (2 * sp + (lead & 1)).astype(F32)
    wmap[...] = (
        gauss(lax.shift_right_logical(lead, 3).astype(F32), PZ) * gauss(row_y, PY) * gauss(width.astype(F32), PX)
    )

    r48 = iota((48, 128), 0)
    c48 = iota((48, 128), 1)
    z48 = lax.shift_right_logical(r48 * 43, 8)
    m48 = r48 - z48 * 6
    for q in range(NP):
        hit = ((c48 & 7) == m48) & (lax.shift_right_logical(c48, 3) == z48 + 8 * q - oz)
        place[q * 48 : q * 48 + 48, :] = jnp.where(hit, 1.0, 0.0).astype(BF)

    rc = iota((48, VX), 0)
    xc = iota((48, VX), 1)
    zc = lax.shift_right_logical(rc * 43, 8)
    yc = (2 * sp + ((rc - zc * 6) & 1)).astype(F32)
    plane = jnp.zeros((48, VX), F32)
    for p in range(NP):
        rel_z = 8 * me + zc - offs[p, 0]
        rel_x = xc - offs[p, 1]
        inside = (rel_z >= 0) & (rel_z < PZ) & (rel_x >= 0) & (rel_x < PX)
        value = gauss(rel_z.astype(F32), PZ) * gauss(rel_x.astype(F32), PX)
        plane = plane + jnp.where(inside, value, 0.0)
    inv[...] = jnp.maximum(plane * gauss(yc, PY), 0.1)

    back = iota((PX, VX), 1) - iota((PX, VX), 0)
    for p in range(NP):
        unblend[p * PX : p * PX + PX, :] = jnp.where(back == offs[p, 1], 1.0, 0.0).astype(BF)

    wait_stats(st1, s_st1, r_st1)
    factor1, shift1 = scales(st1, g1, b1)

    edge = (jnp.where(sp == 0, 0.0, 1.0), jnp.where(sp == NS - 1, 0.0, 1.0))
    lane_b = iota((CH, PX), 1)
    firsts, seconds = [], []
    for zf in range(2):
        for xf in range(2):
            f = zf * 2 + xf
            scale = factor1[f * 32 : f * 32 + 32]
            shift = shift1[f * 32 : f * 32 + 32]
            for zo in range(4):
                for row in range(4):
                    source = own if row in (1, 2) else halo
                    r = row - 1 if row in (1, 2) else row // 3
                    at = zf * 256 + zo * 64 + r * 32
                    if row in (0, 3):
                        sc, sh = scale * edge[row // 3], shift * edge[row // 3]
                    else:
                        sc, sh = scale, shift
                    zp = zo % 2
                    zi = 1 - zp if zf else zp
                    for b in range(4):
                        j = 2 * b + zo // 2
                        u = leaky(source[at : at + 32, xf * 512 + b * PX : xf * 512 + b * PX + PX] * sc + sh)
                        prior = jnp.where(lane_b == 0, 0.0, pltpu.roll(u, 1, 1))
                        later = jnp.where(lane_b == PX - 1, 0.0, pltpu.roll(u, PX - 1, 1))
                        for c, cells in enumerate((prior, u, later)):
                            ci = 2 - c if xf else c
                            k = ((zi * 4 + row) * 3 + ci) * 32
                            act[k : k + 32, f * 1024 + j * PX : f * 1024 + j * PX + PX] = cells.astype(BF)
            pbuf[...] = jnp.dot(w2s[...], act[:, f * 1024 : f * 1024 + 1024], preferred_element_type=F32)

            def slot(s, j):
                s = 3 - s if zf else s
                return pbuf[s * 64 : s * 64 + 64, j * PX : j * PX + PX]

            parts = []
            for j in range(8):
                even = slot(1, j)
                if j > 0:
                    even = even + slot(3, j - 1)
                odd = slot(2, j)
                if j < 7:
                    odd = odd + slot(0, j + 1)
                for zp, value in enumerate((even, odd)):
                    at = f * 128 + zp * 64
                    conv[at : at + 64, j * PX : j * PX + PX] = value
                    parts.append(value[:32])
                    parts.append(value[32:])
            one, two = sums(parts)
            firsts.append(one)
            seconds.append(two)

    st2[sp] = jnp.concatenate([to_lanes(firsts), to_lanes(seconds)], axis=0)
    send_stats(st2, s_st2, r_st2)
    wait_stats(st2, s_st2, r_st2)
    factor2, shift2 = scales(st2, g2, b2)

    for f in range(4):
        scale = factor2[f * 32 : f * 32 + 32]
        shift = shift2[f * 32 : f * 32 + 32]
        for i in range(4):
            at = f * 128 + i * 32
            for j in range(8):
                u = leaky(conv[at : at + 32, j * PX : j * PX + PX] * scale + shift)
                hid[at : at + 32, j * PX : j * PX + PX] = u.astype(BF)
    raw = jnp.dot(whs[...], hid[...], preferred_element_type=F32)
    k_of = lax.shift_right_logical(iota((16, PX), 0) & 7, 1)
    head_b = jnp.where(k_of == 0, hb[0], jnp.where(k_of == 1, hb[1], hb[2]))
    for j in range(8):
        value = (raw[:, j * PX : j * PX + PX] * 0.25 + head_b) * wmap[j * 16 : j * 16 + 16, :]
        logit[j * 16 : j * 16 + 16, :] = value.astype(BF)
    placed = jnp.dot(place[...], logit[...], preferred_element_type=F32)
    for q in range(NP):
        msend[q] = placed[q * 48 : q * 48 + 48].astype(BF)

    def out_copy(q):
        return pltpu.make_async_remote_copy(
            src_ref=msend.at[q], dst_ref=mrecv.at[me],
            send_sem=s_out.at[q], recv_sem=r_out.at[me],
            device_id=(q, sp), device_id_type=MESH,
        )

    def out_arrival(q):
        return pltpu.make_async_remote_copy(
            src_ref=msend.at[q], dst_ref=mrecv.at[q],
            send_sem=s_out.at[q], recv_sem=r_out.at[q],
            device_id=(q, sp), device_id_type=MESH,
        )

    def send_out(k, c):
        out_copy(group(k)).start()
        return c

    lax.fori_loop(1, NP, send_out, 0)
    mrecv[me] = msend[me]

    def wait_out(k, c):
        out_arrival(group(k)).wait_recv()
        return c

    lax.fori_loop(1, NP, wait_out, 0)
    got = jnp.concatenate([mrecv[p] for p in range(NP)], axis=1)
    final = jnp.dot(got, unblend[...], preferred_element_type=F32) / inv[...]
    for z in range(8):
        for k in range(3):
            out[z, k] = final[z * 6 + k * 2 : z * 6 + k * 2 + 2, :]

    def drain_images(k, c):
        image_copy(0, group(k)).wait_send()
        image_copy(2, group(k)).wait_send()
        image_copy(1, group(k)).wait_send()
        return c

    lax.fori_loop(1, NP, drain_images, 0)
    image_copy(0, me).wait_send()
    image_copy(2, me).wait_send()

    def drain_stats(k, c):
        stat_copy(st1, s_st1, r_st1, k).wait_send()
        stat_copy(st2, s_st2, r_st2, k).wait_send()
        return c

    lax.fori_loop(1, NS, drain_stats, 0)

    def drain_out(k, c):
        out_copy(group(k)).wait_send()
        return c

    lax.fori_loop(1, NP, drain_out, 0)


def local(image, offsets, w1, w2, g1, b1, g2, b2, hw, hb):
    vm = pl.BlockSpec(memory_space=pltpu.VMEM)
    sm = pl.BlockSpec(memory_space=pltpu.SMEM)
    dma = pltpu.SemaphoreType.DMA
    return pl.pallas_call(
        kernel,
        out_shape=jax.ShapeDtypeStruct((8, 3, 2, VX), F32),
        in_specs=[vm, sm, vm, vm, vm, vm, vm, vm, vm, sm],
        out_specs=vm,
        scratch_shapes=[
            pltpu.VMEM((16, VX), F32),
            pltpu.VMEM((NP, 16, PX), BF),
            pltpu.VMEM((3, NP, 16, PX), BF),
            pltpu.VMEM((1024, 144), BF),
            pltpu.VMEM((256, 768), BF),
            pltpu.VMEM((16, 512), BF),
            pltpu.VMEM((192, 384), BF),
            pltpu.VMEM((144, 1024), BF),
            pltpu.VMEM((512, 1024), F32),
            pltpu.VMEM((512, 1024), F32),
            pltpu.VMEM((768, 4096), BF),
            pltpu.VMEM((256, 1024), F32),
            pltpu.VMEM((512, 1024), F32),
            pltpu.VMEM((512, 1024), BF),
            pltpu.VMEM((NS, 2, PX), F32),
            pltpu.VMEM((NS, 2, PX), F32),
            pltpu.VMEM((1024, VX), BF),
            pltpu.VMEM((384, PX), BF),
            pltpu.VMEM((48, VX), F32),
            pltpu.VMEM((128, PX), F32),
            pltpu.VMEM((128, PX), BF),
            pltpu.VMEM((NP, 48, PX), BF),
            pltpu.VMEM((NP, 48, PX), BF),
            dma((3, NP)), dma((3, NP)),
            dma((NS,)), dma((NS,)), dma((NS,)), dma((NS,)),
            dma((NP,)), dma((NP,)),
        ],
        compiler_params=pltpu.CompilerParams(collective_id=0, has_side_effects=True, vmem_limit_bytes=60 * 1024 * 1024),
    )(
        image, offsets, w1, w2, g1.reshape(1, CH), b1.reshape(1, CH), g2.reshape(1, CH), b2.reshape(1, CH), hw, hb,
    )


def solution(mesh):
    return jax.shard_map(
        local,
        mesh=mesh,
        in_specs=(P("patch", "space", None), P(), P(), P(), P(), P(), P(), P(), P(), P()),
        out_specs=P("patch", None, "space", None),
        check_vma=False,
    )
```

time: 116 us -> 45.8 us (0.39)
  starting transfers between devices: 45.3 us -> 0 us
  Pallas kernels: 0 us -> 42 us
  waiting for transfers between devices: 36.1 us -> 0 us
  matrix products: 12.3 us -> 0 us
  local copies, waits for them, and re-layouts: 10.9 us -> 3.54 us
  other arithmetic: 5.31 us -> 0 us
  between operations: 4.89 us -> 0.01 us
    pallas_call x0 -> x1, Pallas kernels: none -> 42 us  [local(): pl.pallas_call(kernel, out_shape=jax.ShapeDtypeStruct((8, 3, 2, VX), F32)...]
    all_to_all x4 -> x0, starting transfers between devices: 37.8 us -> none  [the longest x3 27.6 us: copy_for_each(): return lax.all_to_all(copies, axis, split_axis=0, concat_axis=0, tiled=True)]
    all_to_all x4 -> x0, waiting for transfers between devices: 25 us -> none  [the longest x3 17.6 us: copy_for_each(): return lax.all_to_all(copies, axis, split_axis=0, concat_axis=0, tiled=True)]
    dot_general x20 -> x0, matrix products: 12.3 us -> none  [the longest x18 11.4 us: apply_taps(): jnp.einsum('oc,fczyx->fozyx', weights[depth_tap * 3 + row_tap], window, p...]
    ppermute x4 -> x0, waiting for transfers between devices: 11.2 us -> none  [the longest x2 5.94 us: padded_2(): lax.ppermute(tail, axis, [(i, (i + 1) % count) for i in range(ends)])]
    ppermute x4 -> x0, starting transfers between devices: 7.52 us -> none  [the longest x2 4.76 us: padded_2(): lax.ppermute(tail, axis, [(i, (i + 1) % count) for i in range(ends)])]
    concatenate x5 -> x0, other arithmetic: 4.04 us -> none  [the longest x2 3.22 us: padded_2(): jnp.concatenate([lax.ppermute(tail, axis, [(i, (i + 1) % count) for i in...]
    slice x5 -> x0, local copies, waits for them, and re-layouts: 3.16 us -> none  [the longest x2 2.46 us: apply_taps(): padded[:, :, :, :, col_shift:col_shift + col_cells]]
  transfers between devices with their start and end apart: 8 -> 0, of which waited for: 7 -> 0; matrix products, arithmetic and copies ran while one was open for 2% -> 0% of each run, Pallas kernels for 0% -> 0%
where the time goes in v1:
time: 45.8 us; the launch traced here: 45.6 us
  Pallas kernels  42 us (92%)
  local copies, waits for them, and re-layouts  3.54 us (8%)
    pallas_call x1, Pallas kernels, local(): pl.pallas_call(kernel, out_shape=jax.ShapeDtypeStruct((8, 3, 2, VX), F32)...  42 us
    unnamed x5, local copies, waits for them, and re-layouts  3.54 us

profile of v1, /device:TPU:1, one launch (start us, length us, event | category | flops | bytes accessed | tf_op | source)
XLA Modules:
  0.0 45.6 jit_solution(16780193195462160978)
XLA Ops:
  0.0 0.0 copy-start
  0.0 1.4 %copy.11.offs = s32[8,2]{1,0:T(8,128)} copy(s32[8,2]{0,1:T(2,128)} %param.11) | data formatting | bytes 128 | tf_op args[1]
  1.4 0.0 copy-done
  1.4 0.8 %copy.12.w1 = bf16[9,32,3]{2,1,0:T(8,128)(2,1)} copy(bf16[9,32,3]{1,2,0:T(4,128)(2,1)S(1)} %copy-done) | data formatting | bytes 3456 | tf_op args[2]
  2.1 42.0 %shard_map.100 = f32[8,3,2,256]{3,2,1,0:T(2,128)} custom-call(bf16[8,2,256]{2,1,0:T(2,128)(2,1)} %image.1, s32[8,2]{1,0:T(8,128)} %copy.11.offs, bf16[9,32,3]{2,1,0:T(8,128)(2,1)} %copy.12.w1, bf16[9,32,96]{2,1,0:T(8,128)(2,1)} %w2.1, f32[1,32]{1,0:T(1,128)} %bitcast.4, f32[1,32]{1,0:T(1,128)} %bitcast.5, f32[1,32]{1,0:T(1,128)} %bitcast.6, ...), custom_call_target="tpu_custom_call" | custom-call | tf_op jit(solution)/shard_map/pallas_call | solution.py:415
  44.1 1.4 %copy.14 = f32[8,3,2,256]{3,2,1,0:T(2,128)} copy(f32[8,3,2,256]{3,2,1,0:T(2,128)} %shard_map.100) | data formatting | bytes 98304
Async XLA Ops:
  0.0 1.4 %copy-start = (bf16[9,32,3]{1,2,0:T(4,128)(2,1)S(1)}, bf16[9,32,3]{1,2,0:T(4,128)(2,1)}, u32[]{:S(2)}) copy-start(bf16[9,32,3]{1,2,0:T(4,128)(2,1)} %param.12) | copy-start | bytes 5188

commit v2 on v1

--- a/solution.py
+++ b/solution.py
@@ -29,11 +29,16 @@
     return jnp.exp(-(offset * offset) / (2.0 * deviation * deviation))
 
 
+def far(k):
+    dz = (k + 1) // 4
+    return -min(dz, 8 - dz) - min(k % 4, 4 - k % 4)
+
+
 def kernel(
-    image, offs, w1, w2, g1, b1, g2, b2, hw, hb, out,
-    slab, xsend, gath, w1s, w2s, whs, sels, im2, own, halo, act, pbuf, conv, hid,
-    st1, st2, unblend, place, inv, wmap, logit, msend, mrecv,
-    s_img, r_img, s_st1, r_st1, s_st2, r_st2, s_out, r_out,
+    image_in, offs_in, w1_in, w2_in, g1_in, b1_in, g2_in, b2_in, hw_in, hb_in, mrecv, unblend, inv,
+    image, offs, w1, w2, g1, b1, g2, b2, hw, hb, wrow, slab, xsend, gath, w1s, w2s, whs, sels, im2, own, halo, act, pbuf, conv, hid,
+    st1, st2, place, wmap, logit, msend,
+    s_in, s_img, r_img, s_st1, r_st1, s_st2, r_st2, s_out, r_out,
 ):
     me = lax.axis_index("patch")
     sp = lax.axis_index("space")
@@ -49,25 +54,29 @@
     def greet(p, s):
         pl.semaphore_signal(barrier, inc=1, device_id=(p, s), device_id_type=MESH)
 
-    def greet_space(k, c):
+    for k in sorted(range(1, NS), key=far):
         greet(me, space(k))
-        return c
-
-    lax.fori_loop(1, NS, greet_space, 0)
-
-    def greet_group(k, c):
-        greet(group(k), sp)
+    for k in (4, 5, 3, 2, 6, 7, 1):
         greet(group(k), space(1))
         greet(group(k), space(-1))
-        return c
-
-    lax.fori_loop(1, NP, greet_group, 0)
+        greet(group(k), sp)
+
+    pairs = (
+        (image_in, image), (offs_in, offs), (w1_in, w1), (w2_in, w2), (g1_in, g1),
+        (b1_in, b1), (g2_in, g2), (b2_in, b2), (hw_in, hw), (hb_in, hb),
+    )
+    loads = [pltpu.make_async_copy(src, dst, s_in.at[i]) for i, (src, dst) in enumerate(pairs)]
+    for load in loads:
+        load.start()
+    wrow[...] = jnp.zeros_like(wrow)
+    for load in loads[:2]:
+        load.wait()
 
     for z in range(8):
         slab[2 * z : 2 * z + 2, :] = image[z].astype(F32)
     diff = iota((VX, PX), 0) - iota((VX, PX), 1)
     for p in range(NP):
-        pick = jnp.where(diff == offs[p, 1], 1.0, 0.0).astype(BF)
+        pick = jnp.where(diff == offs[1, p], 1.0, 0.0).astype(BF)
         xsend[p] = jnp.dot(slab[...].astype(BF), pick, preferred_element_type=F32).astype(BF)
 
     pl.semaphore_wait(barrier, NS - 1 + 3 * (NP - 1))
@@ -97,15 +106,22 @@
     image_copy(2, me).start()
     gath[1, me] = xsend[me]
 
+    for load in loads[2:]:
+        load.wait()
+    for t in range(9):
+        wrow[3 * t : 3 * t + 3, :] = w1[t].astype(F32)
     lane = iota((CH, VX), 1)
+    tap = iota((CH, VX), 0)
+    tap_a = lax.shift_right_logical(tap * 57, 9)
+    tap_r = tap - 9 * tap_a
+    tap_b = lax.shift_right_logical(tap_r * 11, 5)
+    tap_c = tap_r - 3 * tap_b
     for flip in range(2):
-        base = jnp.zeros((CH, VX), F32)
-        for a in range(3):
-            for b in range(3):
-                taps = w1[3 * a + b].astype(F32)
-                for c in range(3):
-                    where = c * 48 + b * 8 + (2 - a if flip else a)
-                    base = base + jnp.where(lane == where, taps[:, c : c + 1], 0.0)
+        where = tap_c * 48 + tap_b * 8 + (2 - tap_a if flip else tap_a)
+        pick = jnp.where((lane == where) & (tap < 27), 1.0, 0.0).astype(BF)
+        base = lax.dot_general(
+            wrow[...].astype(BF), pick, (((0,), (0,)), ((), ())), preferred_element_type=F32
+        )
         for part in range(2):
             for zo in range(4):
                 for r in range(2):
@@ -128,7 +144,7 @@
     for slot, zp in ((3, 0), (0, 1)):
         w2s[slot * 64 : slot * 64 + 64, zp * 384 : zp * 384 + 384] = jnp.zeros((64, 384), BF)
 
-    oz = offs[me, 0]
+    oz = offs[0, me]
     rows = iota((48, 384), 0)
     cols = iota((48, 384), 1)
     slot_n = lax.shift_right_logical(cols, 7)
@@ -200,10 +216,8 @@
         )
 
     def send_stats(buf, ssem, rsem):
-        def body(k, c):
-            stat_copy(buf, ssem, rsem, lax.rem(k + 15, NS - 1) + 1).start()
-            return c
-        lax.fori_loop(0, NS - 1, body, 0)
+        for k in sorted(range(1, NS), key=far):
+            stat_copy(buf, ssem, rsem, k).start()
 
     def wait_stats(buf, ssem, rsem):
         def body(k, c):
@@ -264,8 +278,8 @@
     yc = (2 * sp + ((rc - zc * 6) & 1)).astype(F32)
     plane = jnp.zeros((48, VX), F32)
     for p in range(NP):
-        rel_z = 8 * me + zc - offs[p, 0]
-        rel_x = xc - offs[p, 1]
+        rel_z = 8 * me + zc - offs[0, p]
+        rel_x = xc - offs[1, p]
         inside = (rel_z >= 0) & (rel_z < PZ) & (rel_x >= 0) & (rel_x < PX)
         value = gauss(rel_z.astype(F32), PZ) * gauss(rel_x.astype(F32), PX)
         plane = plane + jnp.where(inside, value, 0.0)
@@ -273,7 +287,7 @@
 
     back = iota((PX, VX), 1) - iota((PX, VX), 0)
     for p in range(NP):
-        unblend[p * PX : p * PX + PX, :] = jnp.where(back == offs[p, 1], 1.0, 0.0).astype(BF)
+        unblend[p * PX : p * PX + PX, :] = jnp.where(back == offs[1, p], 1.0, 0.0).astype(BF)
 
     wait_stats(st1, s_st1, r_st1)
     factor1, shift1 = scales(st1, g1, b1)
@@ -373,51 +387,73 @@
     lax.fori_loop(1, NP, send_out, 0)
     mrecv[me] = msend[me]
 
+    def drain_images(k, c):
+        image_copy(0, group(k)).wait_send()
+        image_copy(2, group(k)).wait_send()
+        image_copy(1, group(k)).wait_send()
+        return c
+
+    lax.fori_loop(1, NP, drain_images, 0)
+    image_copy(0, me).wait_send()
+    image_copy(2, me).wait_send()
+
+    def drain_stats(k, c):
+        stat_copy(st1, s_st1, r_st1, k).wait_send()
+        stat_copy(st2, s_st2, r_st2, k).wait_send()
+        return c
+
+    lax.fori_loop(1, NS, drain_stats, 0)
+
+    def drain_out(k, c):
+        out_copy(group(k)).wait_send()
+        return c
+
+    lax.fori_loop(1, NP, drain_out, 0)
+
     def wait_out(k, c):
         out_arrival(group(k)).wait_recv()
         return c
 
     lax.fori_loop(1, NP, wait_out, 0)
+
+
+def place_kernel(mrecv, unblend, inv, out):
     got = jnp.concatenate([mrecv[p] for p in range(NP)], axis=1)
     final = jnp.dot(got, unblend[...], preferred_element_type=F32) / inv[...]
     for z in range(8):
         for k in range(3):
             out[z, k] = final[z * 6 + k * 2 : z * 6 + k * 2 + 2, :]
 
-    def drain_images(k, c):
-        image_copy(0, group(k)).wait_send()
-        image_copy(2, group(k)).wait_send()
-        image_copy(1, group(k)).wait_send()
-        return c
-
-    lax.fori_loop(1, NP, drain_images, 0)
-    image_copy(0, me).wait_send()
-    image_copy(2, me).wait_send()
-
-    def drain_stats(k, c):
-        stat_copy(st1, s_st1, r_st1, k).wait_send()
-        stat_copy(st2, s_st2, r_st2, k).wait_send()
-        return c
-
-    lax.fori_loop(1, NS, drain_stats, 0)
-
-    def drain_out(k, c):
-        out_copy(group(k)).wait_send()
-        return c
-
-    lax.fori_loop(1, NP, drain_out, 0)
-
 
 def local(image, offsets, w1, w2, g1, b1, g2, b2, hw, hb):
     vm = pl.BlockSpec(memory_space=pltpu.VMEM)
-    sm = pl.BlockSpec(memory_space=pltpu.SMEM)
+    hold = pl.BlockSpec(memory_space=pltpu.HBM)
     dma = pltpu.SemaphoreType.DMA
-    return pl.pallas_call(
+    inputs = (
+        image, offsets.T, w1.transpose(0, 2, 1), w2, g1.reshape(1, CH), b1.reshape(1, CH), g2.reshape(1, CH),
+        b2.reshape(1, CH), hw, hb,
+    )
+    blocks = pl.pallas_call(
         kernel,
-        out_shape=jax.ShapeDtypeStruct((8, 3, 2, VX), F32),
-        in_specs=[vm, sm, vm, vm, vm, vm, vm, vm, vm, sm],
-        out_specs=vm,
+        out_shape=(
+            pltpu.VMEM((NP, 48, PX), BF),
+            pltpu.VMEM((NP * PX, VX), BF),
+            pltpu.VMEM((48, VX), F32),
+        ),
+        in_specs=[hold] * 10,
+        out_specs=(vm, vm, vm),
         scratch_shapes=[
+            pltpu.VMEM((8, 2, VX), BF),
+            pltpu.SMEM((2, NP), jnp.int32),
+            pltpu.VMEM((9, 3, CH), BF),
+            pltpu.VMEM((9, CH, 96), BF),
+            pltpu.VMEM((1, CH), F32),
+            pltpu.VMEM((1, CH), F32),
+            pltpu.VMEM((1, CH), F32),
+            pltpu.VMEM((1, CH), F32),
+            pltpu.VMEM((3, CH), BF),
+            pltpu.SMEM((3,), F32),
+            pltpu.VMEM((CH, CH), F32),
             pltpu.VMEM((16, VX), F32),
             pltpu.VMEM((NP, 16, PX), BF),
             pltpu.VMEM((3, NP, 16, PX), BF),
@@ -434,21 +470,25 @@
             pltpu.VMEM((512, 1024), BF),
             pltpu.VMEM((NS, 2, PX), F32),
             pltpu.VMEM((NS, 2, PX), F32),
-            pltpu.VMEM((1024, VX), BF),
             pltpu.VMEM((384, PX), BF),
-            pltpu.VMEM((48, VX), F32),
             pltpu.VMEM((128, PX), F32),
             pltpu.VMEM((128, PX), BF),
             pltpu.VMEM((NP, 48, PX), BF),
-            pltpu.VMEM((NP, 48, PX), BF),
-            dma((3, NP)), dma((3, NP)),
+            dma((10,)), dma((3, NP)), dma((3, NP)),
             dma((NS,)), dma((NS,)), dma((NS,)), dma((NS,)),
             dma((NP,)), dma((NP,)),
         ],
-        compiler_params=pltpu.CompilerParams(collective_id=0, has_side_effects=True, vmem_limit_bytes=60 * 1024 * 1024),
-    )(
-        image, offsets, w1, w2, g1.reshape(1, CH), b1.reshape(1, CH), g2.reshape(1, CH), b2.reshape(1, CH), hw, hb,
-    )
+        compiler_params=pltpu.CompilerParams(
+            collective_id=0, has_side_effects=True, vmem_limit_bytes=40 * 1024 * 1024
+        ),
+    )(*[pltpu.with_memory_space_constraint(value, pltpu.HBM) for value in inputs])
+    return pl.pallas_call(
+        place_kernel,
+        out_shape=jax.ShapeDtypeStruct((8, 3, 2, VX), F32),
+        in_specs=[vm, vm, vm],
+        out_specs=vm,
+        compiler_params=pltpu.CompilerParams(vmem_limit_bytes=8 * 1024 * 1024),
+    )(*[pltpu.with_memory_space_constraint(b, pltpu.VMEM) for b in blocks])
 
 
 def solution(mesh):

time: 45.8 us -> 39.4 us (0.86)
  local copies, waits for them, and re-layouts: 3.54 us -> 0 us
  Pallas kernels: 42 us -> 39.3 us
    unnamed x5 -> x0, local copies, waits for them, and re-layouts: 3.54 us -> none
    pallas_call x1 -> x2, Pallas kernels: 42 us -> 39.3 us  [the longest x1 38.4 us: local(): pl.pallas_call(kernel, out_shape=(pltpu.VMEM((NP, 48, PX), BF), pltpu.VME...]
where the time goes in v2:
time: 39.4 us; the launch traced here: 39.3 us
  Pallas kernels  39.3 us (100%)
    pallas_call x1, Pallas kernels, local(): pl.pallas_call(kernel, out_shape=(pltpu.VMEM((NP, 48, PX), BF), pltpu.VME...  38.4 us
    pallas_call x1, Pallas kernels, local(): pl.pallas_call(place_kernel, out_shape=jax.ShapeDtypeStruct((8, 3, 2, VX)...  0.83 us

profile of v2, /device:TPU:1, one launch (start us, length us, event | category | flops | bytes accessed | tf_op | source)
XLA Modules:
  0.0 39.3 jit_solution(4239729401987828416)
XLA Ops:
  0.0 38.4 %shard_map.100 = (bf16[8,48,128]{2,1,0:T(8,128)(2,1)S(1)}, bf16[1024,256]{1,0:T(8,128)(2,1)S(1)}, f32[48,256]{1,0:T(8,128)S(1)}) custom-call(bf16[8,2,256]{2,1,0:T(2,128)(2,1)} %image_in.1, s32[2,8]{1,0:T(2,128)} %bitcast.7, bf16[9,3,32]{2,1,0:T(4,128)(2,1)} %bitcast.6, bf16[9,32,96]{2,1,0:T(8,128)(2,1)} %w2_in.1, f32[1,32]{1,0:T(1,128)} %bitcast.8, ...), custom_call_target="tpu_custom_call" | custom-call | tf_op jit(solution)/shard_map/pallas_call | solution.py:436
  38.4 0.8 %shard_map.101 = f32[8,3,2,256]{3,2,1,0:T(2,128)} custom-call(bf16[8,48,128]{2,1,0:T(8,128)(2,1)S(1)} %get-tuple-element.8.mrecv, bf16[1024,256]{1,0:T(8,128)(2,1)S(1)} %get-tuple-element.9.unblend, f32[48,256]{1,0:T(8,128)S(1)} %get-tuple-element.10.inv), custom_call_target="tpu_custom_call" | custom-call | tf_op jit(solution)/shard_map/pallas_call | solution.py:485

commit v3 on v2

--- a/solution.py
+++ b/solution.py
@@ -38,7 +38,7 @@
     image_in, offs_in, w1_in, w2_in, g1_in, b1_in, g2_in, b2_in, hw_in, hb_in, mrecv, unblend, inv,
     image, offs, w1, w2, g1, b1, g2, b2, hw, hb, wrow, slab, xsend, gath, w1s, w2s, whs, sels, im2, own, halo, act, pbuf, conv, hid,
     st1, st2, place, wmap, logit, msend,
-    s_in, s_img, r_img, s_st1, r_st1, s_st2, r_st2, s_out, r_out,
+    rounds, s_in, s_img, r_img, s_st1, r_st1, s_st2, r_st2, s_out, r_out,
 ):
     me = lax.axis_index("patch")
     sp = lax.axis_index("space")
@@ -54,12 +54,29 @@
     def greet(p, s):
         pl.semaphore_signal(barrier, inc=1, device_id=(p, s), device_id_type=MESH)
 
-    for k in sorted(range(1, NS), key=far):
-        greet(me, space(k))
-    for k in (4, 5, 3, 2, 6, 7, 1):
-        greet(group(k), space(1))
-        greet(group(k), space(-1))
+    above = sp > 0
+    below = sp < NS - 1
+    layer, rank = lax.div(sp, 4), lax.rem(sp, 4)
+
+    def torus(dz, dy):
+        return lax.rem(layer + dz + 8, 8) * 4 + lax.rem(rank + dy + 4, 4)
+
+    order = (4, 5, 3, 2, 6, 7, 1)
+
+    @pl.when(below)
+    def _():
+        for k in order + (0,):
+            greet(group(k), sp + 1)
+
+    @pl.when(above)
+    def _():
+        for k in order + (0,):
+            greet(group(k), sp - 1)
+
+    for k in order:
         greet(group(k), sp)
+    for dz, dy in ((1, 0), (-1, 0), (0, 1), (0, -1)):
+        greet(me, torus(dz, dy))
 
     pairs = (
         (image_in, image), (offs_in, offs), (w1_in, w1), (w2_in, w2), (g1_in, g1),
@@ -79,7 +96,16 @@
         pick = jnp.where(diff == offs[1, p], 1.0, 0.0).astype(BF)
         xsend[p] = jnp.dot(slab[...].astype(BF), pick, preferred_element_type=F32).astype(BF)
 
-    pl.semaphore_wait(barrier, NS - 1 + 3 * (NP - 1))
+    near = jnp.where(above, NP, 0) + jnp.where(below, NP, 0) + NP - 1 + 4
+    pl.semaphore_wait(barrier, near)
+
+    def tell(i, dz, dy):
+        for sign in (1, -1):
+            pl.semaphore_signal(
+                rounds.at[i], inc=1, device_id=(me, torus(sign * dz, sign * dy)), device_id_type=MESH
+            )
+
+    tell(0, 0, 1)
 
     def image_copy(n, p):
         return pltpu.make_async_remote_copy(
@@ -95,16 +121,27 @@
             device_id=(q, space(1 - n)), device_id_type=MESH,
         )
 
-    def send_images(k, c):
-        image_copy(0, group(k)).start()
-        image_copy(2, group(k)).start()
+    @pl.when(below)
+    def _():
+        for k in order + (0,):
+            image_copy(0, group(k)).start()
+
+    @pl.when(above)
+    def _():
+        for k in order + (0,):
+            image_copy(2, group(k)).start()
+
+    for k in order:
         image_copy(1, group(k)).start()
-        return c
-
-    lax.fori_loop(1, NP, send_images, 0)
-    image_copy(0, me).start()
-    image_copy(2, me).start()
     gath[1, me] = xsend[me]
+
+    @pl.when(jnp.logical_not(above))
+    def _():
+        gath[0] = jnp.zeros_like(gath[0])
+
+    @pl.when(jnp.logical_not(below))
+    def _():
+        gath[2] = jnp.zeros_like(gath[2])
 
     for load in loads[2:]:
         load.wait()
@@ -130,6 +167,8 @@
                     moved = base if shift == 0 else pltpu.roll(base, shift, 1)
                     at = part * 512 + flip * 256 + zo * 64 + r * 32
                     w1s[at : at + 32, :] = moved[:, :144].astype(BF)
+    pl.semaphore_wait(rounds.at[0], 2)
+    tell(1, 1, 0)
     nothing = jnp.zeros((CH, 96), F32)
     for a in range(3):
         taps = [w2[3 * a + b].astype(F32) for b in range(3)]
@@ -144,6 +183,9 @@
     for slot, zp in ((3, 0), (0, 1)):
         w2s[slot * 64 : slot * 64 + 64, zp * 384 : zp * 384 + 384] = jnp.zeros((64, 384), BF)
 
+    pl.semaphore_wait(rounds.at[1], 2)
+    tell(2, 2, 0)
+    pl.semaphore_signal(rounds.at[2], inc=1, device_id=(me, torus(2, 1)), device_id_type=MESH)
     oz = offs[0, me]
     rows = iota((48, 384), 0)
     cols = iota((48, 384), 1)
@@ -159,14 +201,22 @@
         hit = keep_row & (from_z == rel + oz) & (rel >= 0) & (rel < PZ)
         sels[b * 48 : b * 48 + 48, :] = jnp.where(hit, 1.0, 0.0).astype(BF)
 
-    for n in range(3):
-        def wait_image(q, c, n=n):
-            image_arrival(n, q).wait_recv()
+    def wait_images(n, first):
+        def body(k, c):
+            image_arrival(n, group(k)).wait_recv()
             return c
-        if n == 1:
-            lax.fori_loop(1, NP, lambda k, c: wait_image(group(k), c), 0)
-        else:
-            lax.fori_loop(0, NP, wait_image, 0)
+
+        lax.fori_loop(first, NP, body, 0)
+
+    wait_images(1, 1)
+
+    @pl.when(above)
+    def _():
+        wait_images(0, 0)
+
+    @pl.when(below)
+    def _():
+        wait_images(2, 0)
 
     rowsel = jnp.dot(sels[...], gath[...].reshape(384, PX), preferred_element_type=F32)
     lane_r = iota((192, PX), 1)
@@ -241,6 +291,7 @@
         return jnp.maximum(u, 0.01 * u)
 
     st1[sp] = jnp.concatenate([to_lanes(firsts), to_lanes(seconds)], axis=0)
+    pl.semaphore_wait(rounds.at[2], 3)
     send_stats(st1, s_st1, r_st1)
 
     halo[...] = jnp.dot(w1s[512:], im2[...], preferred_element_type=F32)
@@ -387,15 +438,22 @@
     lax.fori_loop(1, NP, send_out, 0)
     mrecv[me] = msend[me]
 
-    def drain_images(k, c):
-        image_copy(0, group(k)).wait_send()
-        image_copy(2, group(k)).wait_send()
-        image_copy(1, group(k)).wait_send()
-        return c
-
-    lax.fori_loop(1, NP, drain_images, 0)
-    image_copy(0, me).wait_send()
-    image_copy(2, me).wait_send()
+    def drain_images(n, first):
+        def body(k, c):
+            image_copy(n, group(k)).wait_send()
+            return c
+
+        lax.fori_loop(first, NP, body, 0)
+
+    drain_images(1, 1)
+
+    @pl.when(below)
+    def _():
+        drain_images(0, 0)
+
+    @pl.when(above)
+    def _():
+        drain_images(2, 0)
 
     def drain_stats(k, c):
         stat_copy(st1, s_st1, r_st1, k).wait_send()
@@ -474,6 +532,7 @@
             pltpu.VMEM((128, PX), F32),
             pltpu.VMEM((128, PX), BF),
             pltpu.VMEM((NP, 48, PX), BF),
+            pltpu.SemaphoreType.REGULAR((3,)),
             dma((10,)), dma((3, NP)), dma((3, NP)),
             dma((NS,)), dma((NS,)), dma((NS,)), dma((NS,)),
             dma((NP,)), dma((NP,)),

time: 39.4 us -> 38.6 us (0.980)
  Pallas kernels: 39.3 us -> 38.5 us
    pallas_call x1, Pallas kernels: 38.4 us -> 37.6 us  [local(): pl.pallas_call(kernel, out_shape=(pltpu.VMEM((NP, 48, PX), BF), pltpu.VME...]
where the time goes in v3:
time: 38.6 us; the launch traced here: 38.5 us
  Pallas kernels  38.5 us (100%)
    pallas_call x1, Pallas kernels, local(): pl.pallas_call(kernel, out_shape=(pltpu.VMEM((NP, 48, PX), BF), pltpu.VME...  37.6 us
    pallas_call x1, Pallas kernels, local(): pl.pallas_call(place_kernel, out_shape=jax.ShapeDtypeStruct((8, 3, 2, VX)...  0.83 us

profile of v3, /device:TPU:1, one launch (start us, length us, event | category | flops | bytes accessed | tf_op | source)
XLA Modules:
  0.0 38.5 jit_solution(5479280947247171009)
XLA Ops:
  0.0 37.6 %shard_map.100 = (bf16[8,48,128]{2,1,0:T(8,128)(2,1)S(1)}, bf16[1024,256]{1,0:T(8,128)(2,1)S(1)}, f32[48,256]{1,0:T(8,128)S(1)}) custom-call(bf16[8,2,256]{2,1,0:T(2,128)(2,1)} %image_in.1, s32[2,8]{1,0:T(2,128)} %bitcast.7, bf16[9,3,32]{2,1,0:T(4,128)(2,1)} %bitcast.6, bf16[9,32,96]{2,1,0:T(8,128)(2,1)} %w2_in.1, f32[1,32]{1,0:T(1,128)} %bitcast.8, ...), custom_call_target="tpu_custom_call" | custom-call | tf_op jit(solution)/shard_map/pallas_call | solution.py:494
  37.6 0.8 %shard_map.101 = f32[8,3,2,256]{3,2,1,0:T(2,128)} custom-call(bf16[8,48,128]{2,1,0:T(8,128)(2,1)S(1)} %get-tuple-element.8.mrecv, bf16[1024,256]{1,0:T(8,128)(2,1)S(1)} %get-tuple-element.9.unblend, f32[48,256]{1,0:T(8,128)S(1)} %get-tuple-element.10.inv), custom_call_target="tpu_custom_call" | custom-call | tf_op jit(solution)/shard_map/pallas_call | solution.py:544

commit v4 on v3

--- a/solution.py
+++ b/solution.py
@@ -22,6 +22,10 @@
     return lax.broadcasted_iota(jnp.int32, shape, dim)
 
 
+def wide(ref, blocks):
+    return jnp.concatenate([ref[i] for i in blocks], axis=1)
+
+
 def gauss(positions, length):
     center = (length - 1) / 2.0
     deviation = length / 8.0
@@ -38,7 +42,7 @@
     image_in, offs_in, w1_in, w2_in, g1_in, b1_in, g2_in, b2_in, hw_in, hb_in, mrecv, unblend, inv,
     image, offs, w1, w2, g1, b1, g2, b2, hw, hb, wrow, slab, xsend, gath, w1s, w2s, whs, sels, im2, own, halo, act, pbuf, conv, hid,
     st1, st2, place, wmap, logit, msend,
-    rounds, s_in, s_img, r_img, s_st1, r_st1, s_st2, r_st2, s_out, r_out,
+    late, s_in, s_img, r_img, s_st1, r_st1, s_st2, r_st2, s_out, r_out,
 ):
     me = lax.axis_index("patch")
     sp = lax.axis_index("space")
@@ -75,8 +79,29 @@
 
     for k in order:
         greet(group(k), sp)
-    for dz, dy in ((1, 0), (-1, 0), (0, 1), (0, -1)):
-        greet(me, torus(dz, dy))
+    def release(dz, dy):
+        z = lax.rem(layer + dz + 8, 8)
+        y = lax.rem(rank + dy + 4, 4)
+        return jnp.minimum(z, 4) + jnp.minimum(y, 4 - y)
+
+    mine = release(0, 0)
+    others = sorted(
+        ((dz, dy) for dz in range(-3, 5) for dy in range(-1, 3) if (dz, dy) != (0, 0)),
+        key=lambda d: -abs(d[0]) - abs(d[1]),
+    )
+
+    def tell(signal, later):
+        for dz, dy in others:
+            theirs = release(dz, dy)
+
+            @pl.when(theirs >= mine if later else theirs < mine)
+            def _(dz=dz, dy=dy):
+                pl.semaphore_signal(signal, inc=1, device_id=(me, torus(dz, dy)), device_id_type=MESH)
+
+    tell(barrier, True)
+    known = 0
+    for at, count in enumerate((1, 4, 8, 12, 19, 28, 32)):
+        known = jnp.where(mine == at, count, known)
 
     pairs = (
         (image_in, image), (offs_in, offs), (w1_in, w1), (w2_in, w2), (g1_in, g1),
@@ -96,16 +121,8 @@
         pick = jnp.where(diff == offs[1, p], 1.0, 0.0).astype(BF)
         xsend[p] = jnp.dot(slab[...].astype(BF), pick, preferred_element_type=F32).astype(BF)
 
-    near = jnp.where(above, NP, 0) + jnp.where(below, NP, 0) + NP - 1 + 4
-    pl.semaphore_wait(barrier, near)
-
-    def tell(i, dz, dy):
-        for sign in (1, -1):
-            pl.semaphore_signal(
-                rounds.at[i], inc=1, device_id=(me, torus(sign * dz, sign * dy)), device_id_type=MESH
-            )
-
-    tell(0, 0, 1)
+    near = jnp.where(above, NP, 0) + jnp.where(below, NP, 0) + NP - 1
+    pl.semaphore_wait(barrier, near + known - 1)
 
     def image_copy(n, p):
         return pltpu.make_async_remote_copy(
@@ -133,6 +150,7 @@
 
     for k in order:
         image_copy(1, group(k)).start()
+    tell(late, False)
     gath[1, me] = xsend[me]
 
     @pl.when(jnp.logical_not(above))
@@ -167,8 +185,6 @@
                     moved = base if shift == 0 else pltpu.roll(base, shift, 1)
                     at = part * 512 + flip * 256 + zo * 64 + r * 32
                     w1s[at : at + 32, :] = moved[:, :144].astype(BF)
-    pl.semaphore_wait(rounds.at[0], 2)
-    tell(1, 1, 0)
     nothing = jnp.zeros((CH, 96), F32)
     for a in range(3):
         taps = [w2[3 * a + b].astype(F32) for b in range(3)]
@@ -179,13 +195,12 @@
                 slot = zp - a + 2
                 if 0 <= slot < 4:
                     at = (slot * 2 + ro) * 32
-                    w2s[at : at + 32, zp * 384 : zp * 384 + 384] = block
+                    for i in range(3):
+                        w2s[zp * 3 + i, at : at + 32, :] = block[:, i * PX : i * PX + PX]
     for slot, zp in ((3, 0), (0, 1)):
-        w2s[slot * 64 : slot * 64 + 64, zp * 384 : zp * 384 + 384] = jnp.zeros((64, 384), BF)
-
-    pl.semaphore_wait(rounds.at[1], 2)
-    tell(2, 2, 0)
-    pl.semaphore_signal(rounds.at[2], inc=1, device_id=(me, torus(2, 1)), device_id_type=MESH)
+        for i in range(3):
+            w2s[zp * 3 + i, slot * 64 : slot * 64 + 64, :] = jnp.zeros((64, PX), BF)
+
     oz = offs[0, me]
     rows = iota((48, 384), 0)
     cols = iota((48, 384), 1)
@@ -225,8 +240,8 @@
     for c, cells in enumerate((before, rowsel, after)):
         for b in range(4):
             cut = cells[b * 48 : b * 48 + 48].astype(BF)
-            im2[c * 48 : c * 48 + 48, b * PX : b * PX + PX] = cut
-            im2[(2 - c) * 48 : (2 - c) * 48 + 48, 512 + b * PX : 512 + b * PX + PX] = cut
+            im2[b, c * 48 : c * 48 + 48, :] = cut
+            im2[4 + b, (2 - c) * 48 : (2 - c) * 48 + 48, :] = cut
 
     def sums(parts):
         first = parts[0]
@@ -240,7 +255,7 @@
         cells = jnp.concatenate(blocks, axis=0)
         return jnp.sum(jnp.transpose(cells), axis=0, keepdims=True)
 
-    own[...] = jnp.dot(w1s[:512], im2[...], preferred_element_type=F32)
+    own[...] = jnp.dot(w1s[:512], wide(im2, range(8)), preferred_element_type=F32)
     firsts, seconds = [], []
     for zf in range(2):
         for xf in range(2):
@@ -291,10 +306,13 @@
         return jnp.maximum(u, 0.01 * u)
 
     st1[sp] = jnp.concatenate([to_lanes(firsts), to_lanes(seconds)], axis=0)
-    pl.semaphore_wait(rounds.at[2], 3)
+    @pl.when(known < NS)
+    def _():
+        pl.semaphore_wait(late, NS - known)
+
     send_stats(st1, s_st1, r_st1)
 
-    halo[...] = jnp.dot(w1s[512:], im2[...], preferred_element_type=F32)
+    halo[...] = jnp.dot(w1s[512:], wide(im2, range(8)), preferred_element_type=F32)
 
     row16 = iota((16, 512), 0)
     col16 = iota((16, 512), 1)
@@ -345,6 +363,7 @@
 
     edge = (jnp.where(sp == 0, 0.0, 1.0), jnp.where(sp == NS - 1, 0.0, 1.0))
     lane_b = iota((CH, PX), 1)
+    zero_b = jnp.zeros((CH, PX), BF)
     firsts, seconds = [], []
     for zf in range(2):
         for xf in range(2):
@@ -365,13 +384,16 @@
                     for b in range(4):
                         j = 2 * b + zo // 2
                         u = leaky(source[at : at + 32, xf * 512 + b * PX : xf * 512 + b * PX + PX] * sc + sh)
-                        prior = jnp.where(lane_b == 0, 0.0, pltpu.roll(u, 1, 1))
-                        later = jnp.where(lane_b == PX - 1, 0.0, pltpu.roll(u, PX - 1, 1))
+                        u = u.astype(BF)
+                        prior = jnp.where(lane_b == 0, zero_b, pltpu.roll(u, 1, 1))
+                        later = jnp.where(lane_b == PX - 1, zero_b, pltpu.roll(u, PX - 1, 1))
                         for c, cells in enumerate((prior, u, later)):
                             ci = 2 - c if xf else c
                             k = ((zi * 4 + row) * 3 + ci) * 32
-                            act[k : k + 32, f * 1024 + j * PX : f * 1024 + j * PX + PX] = cells.astype(BF)
-            pbuf[...] = jnp.dot(w2s[...], act[:, f * 1024 : f * 1024 + 1024], preferred_element_type=F32)
+                            act[f * 8 + j, k : k + 32, :] = cells
+            pbuf[...] = jnp.dot(
+                wide(w2s, range(6)), wide(act, range(f * 8, f * 8 + 8)), preferred_element_type=F32
+            )
 
             def slot(s, j):
                 s = 3 - s if zf else s
@@ -406,8 +428,8 @@
             at = f * 128 + i * 32
             for j in range(8):
                 u = leaky(conv[at : at + 32, j * PX : j * PX + PX] * scale + shift)
-                hid[at : at + 32, j * PX : j * PX + PX] = u.astype(BF)
-    raw = jnp.dot(whs[...], hid[...], preferred_element_type=F32)
+                hid[j, at : at + 32, :] = u.astype(BF)
+    raw = jnp.dot(whs[...], wide(hid, range(8)), preferred_element_type=F32)
     k_of = lax.shift_right_logical(iota((16, PX), 0) & 7, 1)
     head_b = jnp.where(k_of == 0, hb[0], jnp.where(k_of == 1, hb[1], hb[2]))
     for j in range(8):
@@ -516,23 +538,23 @@
             pltpu.VMEM((NP, 16, PX), BF),
             pltpu.VMEM((3, NP, 16, PX), BF),
             pltpu.VMEM((1024, 144), BF),
-            pltpu.VMEM((256, 768), BF),
+            pltpu.VMEM((6, 256, PX), BF),
             pltpu.VMEM((16, 512), BF),
             pltpu.VMEM((192, 384), BF),
-            pltpu.VMEM((144, 1024), BF),
+            pltpu.VMEM((8, 144, PX), BF),
             pltpu.VMEM((512, 1024), F32),
             pltpu.VMEM((512, 1024), F32),
-            pltpu.VMEM((768, 4096), BF),
+            pltpu.VMEM((32, 768, PX), BF),
             pltpu.VMEM((256, 1024), F32),
             pltpu.VMEM((512, 1024), F32),
-            pltpu.VMEM((512, 1024), BF),
+            pltpu.VMEM((8, 512, PX), BF),
             pltpu.VMEM((NS, 2, PX), F32),
             pltpu.VMEM((NS, 2, PX), F32),
             pltpu.VMEM((384, PX), BF),
             pltpu.VMEM((128, PX), F32),
             pltpu.VMEM((128, PX), BF),
             pltpu.VMEM((NP, 48, PX), BF),
-            pltpu.SemaphoreType.REGULAR((3,)),
+            pltpu.SemaphoreType.REGULAR,
             dma((10,)), dma((3, NP)), dma((3, NP)),
             dma((NS,)), dma((NS,)), dma((NS,)), dma((NS,)),
             dma((NP,)), dma((NP,)),

time: 38.6 us -> 36.5 us (0.946)
  Pallas kernels: 38.5 us -> 36.4 us
    pallas_call x1, Pallas kernels: 37.6 us -> 35.5 us  [local(): pl.pallas_call(kernel, out_shape=(pltpu.VMEM((NP, 48, PX), BF), pltpu.VME...]
where the time goes in v4:
time: 36.5 us; the launch traced here: 36.4 us
  Pallas kernels  36.4 us (100%)
    pallas_call x1, Pallas kernels, local(): pl.pallas_call(kernel, out_shape=(pltpu.VMEM((NP, 48, PX), BF), pltpu.VME...  35.5 us
    pallas_call x1, Pallas kernels, local(): pl.pallas_call(place_kernel, out_shape=jax.ShapeDtypeStruct((8, 3, 2, VX)...  0.83 us

profile of v4, /device:TPU:1, one launch (start us, length us, event | category | flops | bytes accessed | tf_op | source)
XLA Modules:
  0.0 36.4 jit_solution(9155841863618809586)
XLA Ops:
  0.0 35.5 %shard_map.100 = (bf16[8,48,128]{2,1,0:T(8,128)(2,1)S(1)}, bf16[1024,256]{1,0:T(8,128)(2,1)S(1)}, f32[48,256]{1,0:T(8,128)S(1)}) custom-call(bf16[8,2,256]{2,1,0:T(2,128)(2,1)} %image_in.1, s32[2,8]{1,0:T(2,128)} %bitcast.7, bf16[9,3,32]{2,1,0:T(4,128)(2,1)} %bitcast.6, bf16[9,32,96]{2,1,0:T(8,128)(2,1)} %w2_in.1, f32[1,32]{1,0:T(1,128)} %bitcast.8, ...), custom_call_target="tpu_custom_call" | custom-call | tf_op jit(solution)/shard_map/pallas_call | solution.py:516
  35.5 0.8 %shard_map.101 = f32[8,3,2,256]{3,2,1,0:T(2,128)} custom-call(bf16[8,48,128]{2,1,0:T(8,128)(2,1)S(1)} %get-tuple-element.8.mrecv, bf16[1024,256]{1,0:T(8,128)(2,1)S(1)} %get-tuple-element.9.unblend, f32[48,256]{1,0:T(8,128)S(1)} %get-tuple-element.10.inv), custom_call_target="tpu_custom_call" | custom-call | tf_op jit(solution)/shard_map/pallas_call | solution.py:566

commit v5 on v4

--- a/solution.py
+++ b/solution.py
@@ -42,7 +42,7 @@
     image_in, offs_in, w1_in, w2_in, g1_in, b1_in, g2_in, b2_in, hw_in, hb_in, mrecv, unblend, inv,
     image, offs, w1, w2, g1, b1, g2, b2, hw, hb, wrow, slab, xsend, gath, w1s, w2s, whs, sels, im2, own, halo, act, pbuf, conv, hid,
     st1, st2, place, wmap, logit, msend,
-    late, s_in, s_img, r_img, s_st1, r_st1, s_st2, r_st2, s_out, r_out,
+    late, late_x, s_in, s_img, r_img, s_st1, r_st1, s_st2, r_st2, s_out, r_out,
 ):
     me = lax.axis_index("patch")
     sp = lax.axis_index("space")
@@ -67,18 +67,36 @@
 
     order = (4, 5, 3, 2, 6, 7, 1)
 
-    @pl.when(below)
-    def _():
+    def column(k):
+        x = lax.div(group(k), 2)
+        return jnp.minimum(x, 4 - x)
+
+    mine_x = column(0)
+    seen = jnp.where(mine_x == 0, 2, jnp.where(mine_x == 1, 6, 8))
+    blocks = 1 + jnp.where(above, 1, 0) + jnp.where(below, 1, 0)
+
+    def tell_columns(signal, later):
         for k in order + (0,):
-            greet(group(k), sp + 1)
-
-    @pl.when(above)
-    def _():
-        for k in order + (0,):
-            greet(group(k), sp - 1)
-
-    for k in order:
-        greet(group(k), sp)
+            theirs = column(k)
+
+            @pl.when(theirs >= mine_x if later else theirs < mine_x)
+            def _(k=k):
+                def one(s):
+                    pl.semaphore_signal(signal, inc=1, device_id=(group(k), s), device_id_type=MESH)
+
+                @pl.when(below)
+                def _():
+                    one(sp + 1)
+
+                @pl.when(above)
+                def _():
+                    one(sp - 1)
+
+                if k:
+                    one(sp)
+
+    tell_columns(barrier, True)
+
     def release(dz, dy):
         z = lax.rem(layer + dz + 8, 8)
         y = lax.rem(rank + dy + 4, 4)
@@ -121,8 +139,9 @@
         pick = jnp.where(diff == offs[1, p], 1.0, 0.0).astype(BF)
         xsend[p] = jnp.dot(slab[...].astype(BF), pick, preferred_element_type=F32).astype(BF)
 
-    near = jnp.where(above, NP, 0) + jnp.where(below, NP, 0) + NP - 1
-    pl.semaphore_wait(barrier, near + known - 1)
+    pl.semaphore_wait(barrier, seen * blocks - 1 + known - 1)
+    tell_columns(late_x, False)
+    tell(late, False)
 
     def image_copy(n, p):
         return pltpu.make_async_remote_copy(
@@ -138,19 +157,30 @@
             device_id=(q, space(1 - n)), device_id_type=MESH,
         )
 
-    @pl.when(below)
-    def _():
+    def send_images(known_first):
         for k in order + (0,):
-            image_copy(0, group(k)).start()
-
-    @pl.when(above)
-    def _():
-        for k in order + (0,):
-            image_copy(2, group(k)).start()
-
-    for k in order:
-        image_copy(1, group(k)).start()
-    tell(late, False)
+            theirs = column(k)
+
+            @pl.when(theirs <= mine_x if known_first else theirs > mine_x)
+            def _(k=k):
+                @pl.when(below)
+                def _():
+                    image_copy(0, group(k)).start()
+
+                @pl.when(above)
+                def _():
+                    image_copy(2, group(k)).start()
+
+                if k:
+                    image_copy(1, group(k)).start()
+
+    send_images(True)
+
+    @pl.when(seen < NP)
+    def _():
+        pl.semaphore_wait(late_x, (NP - seen) * blocks)
+        send_images(False)
+
     gath[1, me] = xsend[me]
 
     @pl.when(jnp.logical_not(above))
@@ -285,10 +315,8 @@
             stat_copy(buf, ssem, rsem, k).start()
 
     def wait_stats(buf, ssem, rsem):
-        def body(k, c):
+        for k in sorted(range(1, NS), key=far, reverse=True):
             stat_arrival(buf, ssem, rsem, k).wait_recv()
-            return c
-        lax.fori_loop(1, NS, body, 0)
 
     def scales(buf, gain, bias):
         total = jnp.sum(buf[...], axis=0)
@@ -555,6 +583,7 @@
             pltpu.VMEM((128, PX), BF),
             pltpu.VMEM((NP, 48, PX), BF),
             pltpu.SemaphoreType.REGULAR,
+            pltpu.SemaphoreType.REGULAR,
             dma((10,)), dma((3, NP)), dma((3, NP)),
             dma((NS,)), dma((NS,)), dma((NS,)), dma((NS,)),
             dma((NP,)), dma((NP,)),

time: 36.5 us -> 40.5 us (1.11)
  Pallas kernels: 36.4 us -> 40.3 us
    pallas_call x1, Pallas kernels: 35.5 us -> 39.5 us  [local(): pl.pallas_call(kernel, out_shape=(pltpu.VMEM((NP, 48, PX), BF), pltpu.VME...]
where the time goes in v5:
time: 40.5 us; the launch traced here: 40.3 us
  Pallas kernels  40.3 us (100%)
    pallas_call x1, Pallas kernels, local(): pl.pallas_call(kernel, out_shape=(pltpu.VMEM((NP, 48, PX), BF), pltpu.VME...  39.5 us
    pallas_call x1, Pallas kernels, local(): pl.pallas_call(place_kernel, out_shape=jax.ShapeDtypeStruct((8, 3, 2, VX)...  0.83 us

profile of v5, /device:TPU:1, one launch (start us, length us, event | category | flops | bytes accessed | tf_op | source)
XLA Modules:
  0.0 40.3 jit_solution(6682702309191847118)
XLA Ops:
  0.0 39.5 %shard_map.100 = (bf16[8,48,128]{2,1,0:T(8,128)(2,1)S(1)}, bf16[1024,256]{1,0:T(8,128)(2,1)S(1)}, f32[48,256]{1,0:T(8,128)S(1)}) custom-call(bf16[8,2,256]{2,1,0:T(2,128)(2,1)} %image_in.1, s32[2,8]{1,0:T(2,128)} %bitcast.7, bf16[9,3,32]{2,1,0:T(4,128)(2,1)} %bitcast.6, bf16[9,32,96]{2,1,0:T(8,128)(2,1)} %w2_in.1, f32[1,32]{1,0:T(1,128)} %bitcast.8, ...), custom_call_target="tpu_custom_call" | custom-call | tf_op jit(solution)/shard_map/pallas_call | solution.py:544
  39.5 0.8 %shard_map.101 = f32[8,3,2,256]{3,2,1,0:T(2,128)} custom-call(bf16[8,48,128]{2,1,0:T(8,128)(2,1)S(1)} %get-tuple-element.8.mrecv, bf16[1024,256]{1,0:T(8,128)(2,1)S(1)} %get-tuple-element.9.unblend, f32[48,256]{1,0:T(8,128)S(1)} %get-tuple-element.10.inv), custom_call_target="tpu_custom_call" | custom-call | tf_op jit(solution)/shard_map/pallas_call | solution.py:595

commit v6 on v4

--- a/solution.py
+++ b/solution.py
@@ -40,7 +40,7 @@
 
 def kernel(
     image_in, offs_in, w1_in, w2_in, g1_in, b1_in, g2_in, b2_in, hw_in, hb_in, mrecv, unblend, inv,
-    image, offs, w1, w2, g1, b1, g2, b2, hw, hb, wrow, slab, xsend, gath, w1s, w2s, whs, sels, im2, own, halo, act, pbuf, conv, hid,
+    image, offs, w1, w2, g1, b1, g2, b2, hw, hb, wrow, slab, xsend, gath, w1s, w2s, whs, sels, im2, own, halo, act, pone, ptwo, pbuf, conv, hid,
     st1, st2, place, wmap, logit, msend,
     late, s_in, s_img, r_img, s_st1, r_st1, s_st2, r_st2, s_out, r_out,
 ):
@@ -90,15 +90,15 @@
         key=lambda d: -abs(d[0]) - abs(d[1]),
     )
 
-    def tell(signal, later):
-        for dz, dy in others:
+    def tell(signal, later, members):
+        for dz, dy in members:
             theirs = release(dz, dy)
 
             @pl.when(theirs >= mine if later else theirs < mine)
             def _(dz=dz, dy=dy):
                 pl.semaphore_signal(signal, inc=1, device_id=(me, torus(dz, dy)), device_id_type=MESH)
 
-    tell(barrier, True)
+    tell(barrier, True, others)
     known = 0
     for at, count in enumerate((1, 4, 8, 12, 19, 28, 32)):
         known = jnp.where(mine == at, count, known)
@@ -123,6 +123,7 @@
 
     near = jnp.where(above, NP, 0) + jnp.where(below, NP, 0) + NP - 1
     pl.semaphore_wait(barrier, near + known - 1)
+    tell(late, False, others[:12])
 
     def image_copy(n, p):
         return pltpu.make_async_remote_copy(
@@ -150,7 +151,7 @@
 
     for k in order:
         image_copy(1, group(k)).start()
-    tell(late, False)
+    tell(late, False, others[12:])
     gath[1, me] = xsend[me]
 
     @pl.when(jnp.logical_not(above))
@@ -190,16 +191,17 @@
         taps = [w2[3 * a + b].astype(F32) for b in range(3)]
         for ro in range(2):
             pieces = [nothing] + taps if ro else taps + [nothing]
-            block = jnp.concatenate(pieces, axis=1).astype(BF)
+            pair = jnp.concatenate([piece[:, :64] for piece in pieces], axis=1).astype(BF)
+            last = jnp.concatenate([piece[:, 64:] for piece in pieces], axis=1).astype(BF)
             for zp in range(2):
                 slot = zp - a + 2
                 if 0 <= slot < 4:
                     at = (slot * 2 + ro) * 32
-                    for i in range(3):
-                        w2s[zp * 3 + i, at : at + 32, :] = block[:, i * PX : i * PX + PX]
+                    for i in range(2):
+                        w2s[zp * 2 + i, at : at + 32, :] = pair[:, i * PX : i * PX + PX]
+                    w2s[4 + zp, at : at + 32, :] = last
     for slot, zp in ((3, 0), (0, 1)):
-        for i in range(3):
-            w2s[zp * 3 + i, slot * 64 : slot * 64 + 64, :] = jnp.zeros((64, PX), BF)
+        w2s[4 + zp, slot * 64 : slot * 64 + 64, :] = jnp.zeros((64, PX), BF)
 
     oz = offs[0, me]
     rows = iota((48, 384), 0)
@@ -389,15 +391,25 @@
                         later = jnp.where(lane_b == PX - 1, zero_b, pltpu.roll(u, PX - 1, 1))
                         for c, cells in enumerate((prior, u, later)):
                             ci = 2 - c if xf else c
-                            k = ((zi * 4 + row) * 3 + ci) * 32
+                            k = zi * 256 + (row * 2 + ci) * 32 if ci < 2 else 512 + (zi * 4 + row) * 32
                             act[f * 8 + j, k : k + 32, :] = cells
-            pbuf[...] = jnp.dot(
-                wide(w2s, range(6)), wide(act, range(f * 8, f * 8 + 8)), preferred_element_type=F32
-            )
+            tiles = range(f * 8, f * 8 + 8)
+            for i, buf in enumerate((pone, ptwo)):
+                weights = jnp.concatenate([w2s[2 * i + h, i * 64 : i * 64 + 192, :] for h in range(2)], axis=1)
+                cells = jnp.concatenate([act[t, i * 256 : i * 256 + 256, :] for t in tiles], axis=1)
+                buf[...] = jnp.dot(weights, cells, preferred_element_type=F32)
+            cells = jnp.concatenate([act[t, 512:, :] for t in tiles], axis=1)
+            pbuf[...] = jnp.dot(wide(w2s, (4, 5)), cells, preferred_element_type=F32)
 
             def slot(s, j):
                 s = 3 - s if zf else s
-                return pbuf[s * 64 : s * 64 + 64, j * PX : j * PX + PX]
+                x = j * PX
+                value = pbuf[s * 64 : s * 64 + 64, x : x + PX]
+                if s < 3:
+                    value = value + pone[s * 64 : s * 64 + 64, x : x + PX]
+                if s > 0:
+                    value = value + ptwo[s * 64 - 64 : s * 64, x : x + PX]
+                return value
 
             parts = []
             for j in range(8):
@@ -545,6 +557,8 @@
             pltpu.VMEM((512, 1024), F32),
             pltpu.VMEM((512, 1024), F32),
             pltpu.VMEM((32, 768, PX), BF),
+            pltpu.VMEM((192, 1024), F32),
+            pltpu.VMEM((192, 1024), F32),
             pltpu.VMEM((256, 1024), F32),
             pltpu.VMEM((512, 1024), F32),
             pltpu.VMEM((8, 512, PX), BF),

time: 36.5 us -> 36.3 us (level)
  no operation moved by 1% of the time
where the time goes in v6:
time: 36.3 us; the launch traced here: 36.2 us
  Pallas kernels  36.2 us (100%)
    pallas_call x1, Pallas kernels, local(): pl.pallas_call(kernel, out_shape=(pltpu.VMEM((NP, 48, PX), BF), pltpu.VME...  35.3 us
    pallas_call x1, Pallas kernels, local(): pl.pallas_call(place_kernel, out_shape=jax.ShapeDtypeStruct((8, 3, 2, VX)...  0.83 us

profile of v6, /device:TPU:1, one launch (start us, length us, event | category | flops | bytes accessed | tf_op | source)
XLA Modules:
  0.0 36.2 jit_solution(3068862147058522199)
XLA Ops:
  0.0 35.3 %shard_map.100 = (bf16[8,48,128]{2,1,0:T(8,128)(2,1)S(1)}, bf16[1024,256]{1,0:T(8,128)(2,1)S(1)}, f32[48,256]{1,0:T(8,128)S(1)}) custom-call(bf16[8,2,256]{2,1,0:T(2,128)(2,1)} %image_in.1, s32[2,8]{1,0:T(2,128)} %bitcast.7, bf16[9,3,32]{2,1,0:T(4,128)(2,1)} %bitcast.6, bf16[9,32,96]{2,1,0:T(8,128)(2,1)} %w2_in.1, f32[1,32]{1,0:T(1,128)} %bitcast.8, ...), custom_call_target="tpu_custom_call" | custom-call | tf_op jit(solution)/shard_map/pallas_call | solution.py:528
  35.3 0.8 %shard_map.101 = f32[8,3,2,256]{3,2,1,0:T(2,128)} custom-call(bf16[8,48,128]{2,1,0:T(8,128)(2,1)S(1)} %get-tuple-element.8.mrecv, bf16[1024,256]{1,0:T(8,128)(2,1)S(1)} %get-tuple-element.9.unblend, f32[48,256]{1,0:T(8,128)S(1)} %get-tuple-element.10.inv), custom_call_target="tpu_custom_call" | custom-call | tf_op jit(solution)/shard_map/pallas_call | solution.py:580

commit v7 on v6

--- a/solution.py
+++ b/solution.py
@@ -123,7 +123,7 @@
 
     near = jnp.where(above, NP, 0) + jnp.where(below, NP, 0) + NP - 1
     pl.semaphore_wait(barrier, near + known - 1)
-    tell(late, False, others[:12])
+    tell(late, False, others)
 
     def image_copy(n, p):
         return pltpu.make_async_remote_copy(
@@ -151,7 +151,6 @@
 
     for k in order:
         image_copy(1, group(k)).start()
-    tell(late, False, others[12:])
     gath[1, me] = xsend[me]
 
     @pl.when(jnp.logical_not(above))
@@ -287,9 +286,12 @@
             stat_copy(buf, ssem, rsem, k).start()
 
     def wait_stats(buf, ssem, rsem):
-        def body(k, c):
+        def body(i, c):
+            step = lax.div(i + 1, 2)
+            k = jnp.where(lax.rem(i, 2) == 1, step, NS - step)
             stat_arrival(buf, ssem, rsem, k).wait_recv()
             return c
+
         lax.fori_loop(1, NS, body, 0)
 
     def scales(buf, gain, bias):

time: 36.3 us -> 36.4 us (level)
  no operation moved by 1% of the time
where the time goes in v7:
time: 36.4 us; the launch traced here: 36.2 us
  Pallas kernels  36.2 us (99%)
    pallas_call x1, Pallas kernels, local(): pl.pallas_call(kernel, out_shape=(pltpu.VMEM((NP, 48, PX), BF), pltpu.VME...  35.4 us
    pallas_call x1, Pallas kernels, local(): pl.pallas_call(place_kernel, out_shape=jax.ShapeDtypeStruct((8, 3, 2, VX)...  0.83 us

profile of v7, /device:TPU:1, one launch (start us, length us, event | category | flops | bytes accessed | tf_op | source)
XLA Modules:
  0.0 36.2 jit_solution(3969293166405563245)
XLA Ops:
  0.0 35.4 %shard_map.100 = (bf16[8,48,128]{2,1,0:T(8,128)(2,1)S(1)}, bf16[1024,256]{1,0:T(8,128)(2,1)S(1)}, f32[48,256]{1,0:T(8,128)S(1)}) custom-call(bf16[8,2,256]{2,1,0:T(2,128)(2,1)} %image_in.1, s32[2,8]{1,0:T(2,128)} %bitcast.7, bf16[9,3,32]{2,1,0:T(4,128)(2,1)} %bitcast.6, bf16[9,32,96]{2,1,0:T(8,128)(2,1)} %w2_in.1, f32[1,32]{1,0:T(1,128)} %bitcast.8, ...), custom_call_target="tpu_custom_call" | custom-call | tf_op jit(solution)/shard_map/pallas_call | solution.py:530
  35.4 0.8 %shard_map.101 = f32[8,3,2,256]{3,2,1,0:T(2,128)} custom-call(bf16[8,48,128]{2,1,0:T(8,128)(2,1)S(1)} %get-tuple-element.8.mrecv, bf16[1024,256]{1,0:T(8,128)(2,1)S(1)} %get-tuple-element.9.unblend, f32[48,256]{1,0:T(8,128)S(1)} %get-tuple-element.10.inv), custom_call_target="tpu_custom_call" | custom-call | tf_op jit(solution)/shard_map/pallas_call | solution.py:582
